TPU v7x, 32 devices: a whole 2x2x4 slice. The times are simulated.
32 devices in a mesh: gx: 4 (over x, core), gy: 2 (over y), gz: 4 (over z).
Axes of the slice: x: 2, y: 2, z: 4, core: 2. Of those that a mesh axis runs over, the one named last changes fastest.
Arguments:
- velocity: float32 [3, 512, 512], P(None, None, ('gx', 'gy', 'gz')), may hold values from -4 to 4
- inv_density: float32 [512, 512], P(None, ('gx', 'gy', 'gz')), may hold values from 0.25 to 4
- element_place: int32 [512], P(('gx', 'gy', 'gz')), may hold values from 0 to 15, as said below
Outputs:
- advected: float32 [3, 512, 512], P(None, None, ('gx', 'gy', 'gz'))
- pressure: float32 [512, 512], P(None, ('gx', 'gy', 'gz'))
- residual: float32 [512, 512], P(None, ('gx', 'gy', 'gz'))
Inputs may be any that keep to these rules, and one draw needn't show every extreme that they name: `element_place`: within each device's 16 consecutive elements every block position appears exactly once.
All inputs are finite; a program needn't handle non-finite values.
Results may differ from a plain program's by a relative error of at most 0.0003.
Values sent between devices are 32-bit elements; how exact they have to be, the bound alone decides.
A program may use at most 64 MiB of HBM per device.

v0:
```python
import jax
import jax.numpy as jnp
from jax import lax
from jax.sharding import PartitionSpec as P

BX = 4
BY = 4
BZ = 1
CG_ITERS = 2


time_step = 0.03
mass_shift = 4.0
inner_nodes = (
    -0.8717401485096066,
    -0.5917001814331423,
    -0.2092992179024789,
    0.2092992179024789,
    0.5917001814331423,
    0.8717401485096066,
)


def extended(cells, sides, width):
    for axis, dim in sides:
        count = lax.axis_size(axis)
        ends = count - 1
        head = lax.slice_in_dim(cells, 0, width, axis=dim)
        tail = lax.slice_in_dim(cells, cells.shape[dim] - width, cells.shape[dim], axis=dim)
        cells = jnp.concatenate(
            [
                lax.ppermute(tail, axis, [(i, (i + 1) % count) for i in range(ends)]),
                cells,
                lax.ppermute(head, axis, [((i + 1) % count, i) for i in range(ends)]),
            ],
            axis=dim,
        )
    return cells


def legendre_seven(position):
    previous = 1.0
    current_value = position
    for degree_index in range(1, 7):
        following = (
            (2 * degree_index + 1) * position * current_value - degree_index * previous
        ) / (degree_index + 1)
        previous = current_value
        current_value = following
    return current_value


def tables():
    node_values = [-1.0] + list(inner_nodes) + [1.0]
    poly_values = [legendre_seven(node) for node in node_values]
    weights = [2.0 / (56.0 * value * value) for value in poly_values]
    derivative = [[0.0] * 8 for row_index in range(8)]
    for row_index in range(8):
        for col_index in range(8):
            if row_index != col_index:
                derivative[row_index][col_index] = poly_values[row_index] / (
                    poly_values[col_index] * (node_values[row_index] - node_values[col_index])
                )
    derivative[0][0] = -14.0
    derivative[7][7] = 14.0
    squared_t = [
        [derivative[col_index][row_index] ** 2 for col_index in range(8)] for row_index in range(8)
    ]
    quad_list = [
        weights[first] * weights[second] * weights[third]
        for first in range(8)
        for second in range(8)
        for third in range(8)
    ]
    quadrature = jnp.asarray(quad_list, jnp.float32).reshape(1, 8, 8, 8, 1)
    return (quadrature, jnp.asarray(derivative, jnp.float32), jnp.asarray(squared_t, jnp.float32))


def apply_along(matrix, widened, values, direction):
    if direction == 0:
        return jnp.einsum("ij,sjbk->sibk", matrix, values, precision=lax.Precision.HIGHEST)
    if direction == 1:
        return jnp.einsum("ij,sajk->saik", matrix, values, precision=lax.Precision.HIGHEST)
    return jnp.einsum("ij,sabj->sabi", widened, values, precision=lax.Precision.HIGHEST)


def multiplicity(offsets, totals, block_shape, elements):
    slot_index = jnp.arange(elements, dtype=jnp.int32)
    places = (
        slot_index // (block_shape[1] * block_shape[2]),
        slot_index // block_shape[2] % block_shape[1],
        slot_index % block_shape[2],
    )
    node_index = jnp.arange(8, dtype=jnp.int32)
    first_node = (node_index == 0).astype(jnp.float32)[:, None]
    last_node = (node_index == 7).astype(jnp.float32)[:, None]
    factors = []
    for direction in range(3):
        position = places[direction] + offsets[direction]
        lower_open = (position > 0).astype(jnp.float32)[None, :]
        upper_open = (position < totals[direction] - 1).astype(jnp.float32)[None, :]
        factors.append(1.0 + first_node * lower_open + last_node * upper_open)
    joined = (
        factors[0][:, None, None, :] * factors[1][None, :, None, :] * factors[2][None, None, :, :]
    )
    return joined[None]


def face_take(values, direction, node, block_shape):
    elements = block_shape[0] * block_shape[1] * block_shape[2]
    if direction == 2:
        piece = lax.slice_in_dim(values, node * elements, (node + 1) * elements, axis=3)
    else:
        piece = lax.index_in_dim(values, node, 1 + direction, keepdims=False).reshape(
            values.shape[0], 8, 8, elements
        )
    return piece.reshape(piece.shape[:3] + tuple(block_shape))


def face_write(values, direction, node, piece, elements):
    flat = piece.reshape(piece.shape[:3] + (elements,))
    if direction == 2:
        return lax.dynamic_update_slice_in_dim(values, flat, node * elements, 3)
    widened = jnp.expand_dims(flat.reshape(flat.shape[0], 8, 8 * elements), 1 + direction)
    return lax.dynamic_update_slice_in_dim(values, widened, node, 1 + direction)


def assemble_axis(values, direction, block_shape, sender):
    elements = block_shape[0] * block_shape[1] * block_shape[2]
    lower_faces = face_take(values, direction, 0, block_shape)
    upper_faces = face_take(values, direction, 7, block_shape)
    element_axis = 3 + direction
    length = block_shape[direction]
    interior = lax.slice_in_dim(upper_faces, 0, length - 1, axis=element_axis) + lax.slice_in_dim(
        lower_faces, 1, length, axis=element_axis
    )
    lower_edge = lax.slice_in_dim(lower_faces, 0, 1, axis=element_axis)
    upper_edge = lax.slice_in_dim(upper_faces, length - 1, length, axis=element_axis)
    arrived = sender(jnp.stack([lower_edge, upper_edge]))
    first_sum = lower_edge + arrived[0]
    last_sum = upper_edge + arrived[3]
    new_lower = jnp.concatenate([first_sum, interior], axis=element_axis)
    new_upper = jnp.concatenate([interior, last_sum], axis=element_axis)
    values = face_write(values, direction, 0, new_lower, elements)
    return face_write(values, direction, 7, new_upper, elements)


def send_along_x(face_pair):
    return extended(face_pair, (("gx", 0),), 1)


def send_along_y(face_pair):
    return extended(face_pair, (("gy", 0),), 1)


def send_along_z(face_pair):
    return extended(face_pair, (("gz", 0),), 1)


def assemble(values):
    block_shape = (BX, BY, BZ)
    values = assemble_axis(values, 0, block_shape, send_along_x)
    values = assemble_axis(values, 1, block_shape, send_along_y)
    return assemble_axis(values, 2, block_shape, send_along_z)


def joined_sums(residual, precond, applied_precond, inverse_copies):
    return lax.psum(
        (
            jnp.sum(residual * precond * inverse_copies),
            jnp.sum(precond * applied_precond * inverse_copies),
        ),
        ("gx", "gy", "gz"),
    )


def per_device(velocity, inv_density, element_place):
    elements = element_place.shape[0]
    width = 8 * elements
    quadrature, derivative, square_table = tables()
    identity = jnp.eye(elements, dtype=jnp.float32)
    derivative_wide = jnp.kron(derivative, identity)
    transpose_wide = jnp.kron(derivative.T, identity)
    square_wide = jnp.kron(square_table, identity)
    slot_index = jnp.arange(elements, dtype=jnp.int32)
    inverse = jnp.zeros((elements,), jnp.int32).at[element_place].set(slot_index)
    advector = jnp.take(velocity, inverse, axis=2).reshape(3, 8, 8, width)
    mobility = jnp.take(inv_density, inverse, axis=1).reshape(1, 8, 8, width)
    quad_wide = jnp.broadcast_to(quadrature, (1, 8, 8, 8, elements)).reshape(1, 8, 8, width)
    offsets = (lax.axis_index("gx") * BX, lax.axis_index("gy") * BY, lax.axis_index("gz") * BZ)
    totals = (BX * lax.axis_size("gx"), BY * lax.axis_size("gy"), BZ * lax.axis_size("gz"))
    copies = multiplicity(offsets, totals, (BX, BY, BZ), elements).reshape(1, 8, 8, width)
    mass = quad_wide * copies
    inverse_copies = 1.0 / copies

    def advection_rate(section_value):
        convective = advector[0:1] * apply_along(derivative, derivative_wide, section_value, 0)
        convective = convective + advector[1:2] * apply_along(
            derivative, derivative_wide, section_value, 1
        )
        convective = convective + advector[2:3] * apply_along(
            derivative, derivative_wide, section_value, 2
        )
        return assemble(-quad_wide * convective) / mass

    first_rate = advection_rate(advector)
    second_rate = advection_rate(advector + 0.5 * time_step * first_rate)
    third_rate = advection_rate(advector + 0.5 * time_step * second_rate)
    fourth_rate = advection_rate(advector + time_step * third_rate)
    advected = advector + time_step / 6.0 * (
        first_rate + 2.0 * second_rate + 2.0 * third_rate + fourth_rate
    )
    divergence = (
        apply_along(derivative, derivative_wide, advected[0:1], 0)
        + apply_along(derivative, derivative_wide, advected[1:2], 1)
        + apply_along(derivative, derivative_wide, advected[2:3], 2)
    )
    weighted = quad_wide * mobility
    diag_local = (
        mass_shift * quad_wide
        + apply_along(square_table, square_wide, weighted, 0)
        + apply_along(square_table, square_wide, weighted, 1)
        + apply_along(square_table, square_wide, weighted, 2)
    )
    source_local = -quad_wide * divergence / time_step
    assembled = assemble(jnp.concatenate([source_local, diag_local], axis=0))
    source = assembled[0:1]
    inverse_jacobi = 1.0 / assembled[1:2]

    def operator(values):
        summed = mass_shift * quad_wide * values
        for direction in range(3):
            slope = apply_along(derivative, derivative_wide, values, direction)
            summed = summed + apply_along(derivative.T, transpose_wide, weighted * slope, direction)
        return assemble(summed)

    pressure = jnp.zeros_like(source)
    residual = source
    precond = residual * inverse_jacobi
    applied_precond = operator(precond)
    current, curvature = joined_sums(residual, precond, applied_precond, inverse_copies)
    step_size = current / curvature
    search = precond
    applied_search = applied_precond
    for iteration in range(CG_ITERS):
        pressure = pressure + step_size * search
        residual = residual - step_size * applied_search
        if iteration + 1 < CG_ITERS:
            precond = residual * inverse_jacobi
            applied_precond = operator(precond)
            following, curvature = joined_sums(residual, precond, applied_precond, inverse_copies)
            ratio = following / current
            step_size = following / (curvature - ratio * following / step_size)
            search = precond + ratio * search
            applied_search = applied_precond + ratio * applied_search
            current = following
    advected_out = jnp.take(advected.reshape(3, 512, elements), element_place, axis=2)
    pressure_out = jnp.take(pressure.reshape(512, elements), element_place, axis=1)
    residual_out = jnp.take(residual.reshape(512, elements), element_place, axis=1)
    return (advected_out, pressure_out, residual_out)


def solution(mesh):
    placed = (P(None, None, ("gx", "gy", "gz")), P(None, ("gx", "gy", "gz")), P(("gx", "gy", "gz")))
    return jax.shard_map(
        per_device,
        mesh=mesh,
        in_specs=placed,
        out_specs=(
            P(None, None, ("gx", "gy", "gz")),
            P(None, ("gx", "gy", "gz")),
            P(None, ("gx", "gy", "gz")),
        ),
        check_vma=False,
    )
```

profile of v0, /device:TPU:0, one launch (start us, length us, event | category | flops | bytes accessed | tf_op | source)
XLA Modules:
  0.0 352.7 jit_solution(13022909186866126445)
XLA Ops:
  12.6 1.7 collective-permute-done.1
  14.3 5.5 %collective-permute-start = (f32[1,3,8,8,1,4,1]{2,5,3,1,6,4,0:T(4,128)S(1)}, f32[1,3,8,8,1,4,1]{2,5,3,1,6,4,0:T(4,128)S(1)}, u32[]{:S(2)}, u32[]{:S(2)}) collective-permute-start(f32[1,3,8,8,1,4,1]{2,5,3,1,6,4,0:T(4,128)S(1)} %get-tuple-element.41), channel_id=1, source_target_pairs={{0,8},{8,16},{16,24},{1,9},{9,17},{17,25},{2,10},{10,18},{18,26},{... | collective-permute-start | bytes 9224 | tf_op jit(solution)/shard_map/ppermute | solution.py:32
  22.8 4.5 %collective-permute-done.3 = f32[1,3,8,8,4,1,1]{2,4,3,1,6,5,0:T(4,128)S(1)} collective-permute-done((f32[1,3,8,8,4,1,1]{2,4,3,1,6,5,0:T(4,128)S(1)}, f32[1,3,8,8,4,1,1]{2,4,3,1,6,5,0:T(4,128)S(1)}, u32[]{:S(2)}, u32[]{:S(2)}) %collective-permute-start.3) | collective-permute-done | bytes 3104 | tf_op jit(solution)/shard_map/ppermute | solution.py:34
  27.4 1.7 collective-permute-start.2
  29.3 1.6 collective-permute-done.2
  31.6 3.5 collective-permute-start.4
  38.4 5.4 %collective-permute-done.5 = f32[1,3,8,8,4,4,1]{3,2,5,4,1,6,0:T(8,128)} collective-permute-done((f32[1,3,8,8,4,4,1]{3,2,5,4,1,6,0:T(8,128)}, f32[1,3,8,8,4,4,1]{3,2,5,4,1,6,0:T(8,128)}, u32[]{:S(2)}, u32[]{:S(2)}) %collective-permute-start.5) | collective-permute-done | bytes 12320 | tf_op jit(solution)/shard_map/ppermute | solution.py:34
  45.3 3.6 %dynamic_update_slice.131 = f32[3,8,8,128]{3,1,2,0:T(8,128)S(1)} dynamic-update-slice(f32[3,8,8,128]{3,1,2,0:T(8,128)S(1)} %dynamic_update_slice.130, f32[3,8,8,16]{3,1,2,0:T(8,128)S(1)} %get-tuple-element.82, s32[]{:T(128)} %constant.106.clone.1, s32[]{:T(128)} %constant.106.clone.1, s32[]{:T(128)} %constant.106.clone.1, s32[]{:T(128)} %constant.109.clone.1) | dynamic-update-slice | bytes 24580 | tf_op jit(solution)/shard_map/dynamic_update_slice | solution.py:123
  51.4 1.7 collective-permute-done.7
  53.1 5.1 %collective-permute-start.6 = (f32[1,3,8,8,1,4,1]{2,5,3,1,6,4,0:T(4,128)S(1)}, f32[1,3,8,8,1,4,1]{2,5,3,1,6,4,0:T(4,128)S(1)}, u32[]{:S(2)}, u32[]{:S(2)}) collective-permute-start(f32[1,3,8,8,1,4,1]{2,5,3,1,6,4,0:T(4,128)S(1)} %get-tuple-element.35), channel_id=1, source_target_pairs={{0,8},{8,16},{16,24},{1,9},{9,17},{17,25},{2,10},{10,18},{18,26},{... | collective-permute-start | bytes 9224 | tf_op jit(solution)/shard_map/ppermute | solution.py:32
  61.2 4.6 %collective-permute-done.9 = f32[1,3,8,8,4,1,1]{2,4,3,1,6,5,0:T(4,128)S(1)} collective-permute-done((f32[1,3,8,8,4,1,1]{2,4,3,1,6,5,0:T(4,128)S(1)}, f32[1,3,8,8,4,1,1]{2,4,3,1,6,5,0:T(4,128)S(1)}, u32[]{:S(2)}, u32[]{:S(2)}) %collective-permute-start.9) | collective-permute-done | bytes 3104 | tf_op jit(solution)/shard_map/ppermute | solution.py:34
  69.8 3.5 collective-permute-start.10
  76.6 5.4 %collective-permute-done.11 = f32[1,3,8,8,4,4,1]{3,2,5,4,1,6,0:T(8,128)} collective-permute-done((f32[1,3,8,8,4,4,1]{3,2,5,4,1,6,0:T(8,128)}, f32[1,3,8,8,4,4,1]{3,2,5,4,1,6,0:T(8,128)}, u32[]{:S(2)}, u32[]{:S(2)}) %collective-permute-start.11) | collective-permute-done | bytes 12320 | tf_op jit(solution)/shard_map/ppermute | solution.py:34
  83.6 3.6 %dynamic_update_slice.137 = f32[3,8,8,128]{3,1,2,0:T(8,128)S(1)} dynamic-update-slice(f32[3,8,8,128]{3,1,2,0:T(8,128)S(1)} %dynamic_update_slice.136, f32[3,8,8,16]{3,1,2,0:T(8,128)S(1)} %get-tuple-element.74, s32[]{:T(128)} %constant.106.clone.1, s32[]{:T(128)} %constant.106.clone.1, s32[]{:T(128)} %constant.106.clone.1, s32[]{:T(128)} %constant.109.clone.1) | dynamic-update-slice | bytes 24580 | tf_op jit(solution)/shard_map/dynamic_update_slice | solution.py:123
  90.1 1.8 collective-permute-done.13
  92.8 5.1 %collective-permute-start.12 = (f32[1,3,8,8,1,4,1]{2,5,3,1,6,4,0:T(4,128)S(1)}, f32[1,3,8,8,1,4,1]{2,5,3,1,6,4,0:T(4,128)S(1)}, u32[]{:S(2)}, u32[]{:S(2)}) collective-permute-start(f32[1,3,8,8,1,4,1]{2,5,3,1,6,4,0:T(4,128)S(1)} %get-tuple-element.29), channel_id=1, source_target_pairs={{0,8},{8,16},{16,24},{1,9},{9,17},{17,25},{2,10},{10,18},{18,26},{... | collective-permute-start | bytes 9224 | tf_op jit(solution)/shard_map/ppermute | solution.py:32
  100.8 4.7 %collective-permute-done.15 = f32[1,3,8,8,4,1,1]{2,4,3,1,6,5,0:T(4,128)} collective-permute-done((f32[1,3,8,8,4,1,1]{2,4,3,1,6,5,0:T(4,128)S(1)}, f32[1,3,8,8,4,1,1]{2,4,3,1,6,5,0:T(4,128)}, u32[]{:S(2)}, u32[]{:S(2)}) %collective-permute-start.15) | collective-permute-done | bytes 3104 | tf_op jit(solution)/shard_map/ppermute | solution.py:34
  111.7 3.5 collective-permute-start.16
  116.8 1.8 collective-permute-done.16
  120.4 2.7 collective-permute-done.17
  123.1 1.7 copy.190
  127.4 3.6 %dynamic_update_slice.143 = f32[3,8,8,128]{3,1,2,0:T(8,128)S(1)} dynamic-update-slice(f32[3,8,8,128]{3,1,2,0:T(8,128)S(1)} %dynamic_update_slice.142, f32[3,8,8,16]{3,1,2,0:T(8,128)S(1)} %get-tuple-element.66, s32[]{:T(128)} %constant.106.clone.1, s32[]{:T(128)} %constant.106.clone.1, s32[]{:T(128)} %constant.106.clone.1, s32[]{:T(128)} %constant.109.clone.1) | dynamic-update-slice | bytes 24580 | tf_op jit(solution)/shard_map/dynamic_update_slice | solution.py:123
  134.9 1.7 collective-permute-done.19
  137.5 5.1 %collective-permute-start.18 = (f32[1,3,8,8,1,4,1]{2,5,3,1,6,4,0:T(4,128)S(1)}, f32[1,3,8,8,1,4,1]{2,5,3,1,6,4,0:T(4,128)S(1)}, u32[]{:S(2)}, u32[]{:S(2)}) collective-permute-start(f32[1,3,8,8,1,4,1]{2,5,3,1,6,4,0:T(4,128)S(1)} %get-tuple-element.23), channel_id=1, source_target_pairs={{0,8},{8,16},{16,24},{1,9},{9,17},{17,25},{2,10},{10,18},{18,26},{... | collective-permute-start | bytes 9224 | tf_op jit(solution)/shard_map/ppermute | solution.py:32
  147.2 2.8 collective-permute-done.21
  150.2 1.7 collective-permute-start.20
  154.5 1.9 collective-permute-start.22
  158.2 1.7 collective-permute-done.22
  160.0 4.0 %collective-permute-done.23 = f32[1,3,8,8,4,4,1]{3,2,5,4,1,6,0:T(8,128)S(1)} collective-permute-done((f32[1,3,8,8,4,4,1]{3,2,5,4,1,6,0:T(8,128)S(1)}, f32[1,3,8,8,4,4,1]{3,2,5,4,1,6,0:T(8,128)S(1)}, u32[]{:S(2)}, u32[]{:S(2)}) %collective-permute-start.23) | collective-permute-done | bytes 12320 | tf_op jit(solution)/shard_map/ppermute | solution.py:34
  164.7 3.6 %dynamic_update_slice.149 = f32[3,8,8,128]{3,1,2,0:T(8,128)S(1)} dynamic-update-slice(f32[3,8,8,128]{3,1,2,0:T(8,128)S(1)} %dynamic_update_slice.148, f32[3,8,8,16]{3,1,2,0:T(8,128)S(1)} %get-tuple-element.58, s32[]{:T(128)} %constant.106.clone.1, s32[]{:T(128)} %constant.106.clone.1, s32[]{:T(128)} %constant.106.clone.1, s32[]{:T(128)} %constant.109.clone.1) | dynamic-update-slice | bytes 24580 | tf_op jit(solution)/shard_map/dynamic_update_slice | solution.py:123
  171.3 1.8 collective-permute-done.25
  173.1 4.9 %collective-permute-start.24 = (f32[1,2,8,8,1,4,1]{2,5,3,1,6,4,0:T(4,128)S(1)}, f32[1,2,8,8,1,4,1]{2,5,3,1,6,4,0:T(4,128)S(1)}, u32[]{:S(2)}, u32[]{:S(2)}) collective-permute-start(f32[1,2,8,8,1,4,1]{2,5,3,1,6,4,0:T(4,128)S(1)} %get-tuple-element.55), channel_id=1, source_target_pairs={{0,8},{8,16},{16,24},{1,9},{9,17},{17,25},{2,10},{10,18},{18,26},{... | collective-permute-start | bytes 6152 | tf_op jit(solution)/shard_map/ppermute | solution.py:32
  180.7 4.4 %collective-permute-done.27 = f32[1,2,8,8,4,1,1]{2,4,3,1,6,5,0:T(4,128)S(1)} collective-permute-done((f32[1,2,8,8,4,1,1]{2,4,3,1,6,5,0:T(4,128)S(1)}, f32[1,2,8,8,4,1,1]{2,4,3,1,6,5,0:T(4,128)S(1)}, u32[]{:S(2)}, u32[]{:S(2)}) %collective-permute-start.27) | collective-permute-done | bytes 2080 | tf_op jit(solution)/shard_map/ppermute | solution.py:34
  188.9 1.9 collective-permute-start.28
  193.4 4.4 %collective-permute-done.29 = f32[1,2,8,8,4,4,1]{3,2,5,4,1,6,0:T(8,128)S(1)} collective-permute-done((f32[1,2,8,8,4,4,1]{3,2,5,4,1,6,0:T(8,128)S(1)}, f32[1,2,8,8,4,4,1]{3,2,5,4,1,6,0:T(8,128)S(1)}, u32[]{:S(2)}, u32[]{:S(2)}) %collective-permute-start.29) | collective-permute-done | bytes 8224 | tf_op jit(solution)/shard_map/ppermute | solution.py:34
  198.4 2.5 dynamic_update_slice.155
  203.7 1.7 collective-permute-done.31
  205.4 4.6 %collective-permute-start.30 = (f32[1,1,8,8,1,4,1]{2,5,3,6,4,1,0:T(4,128)S(1)}, f32[1,1,8,8,1,4,1]{2,5,3,6,4,1,0:T(4,128)S(1)}, u32[]{:S(2)}, u32[]{:S(2)}) collective-permute-start(f32[1,1,8,8,1,4,1]{2,5,3,6,4,1,0:T(4,128)S(1)} %get-tuple-element.104), channel_id=1, source_target_pairs={{0,8},{8,16},{16,24},{1,9},{9,17},{17,25},{2,10},{10,18},{18,26},{... | collective-permute-start | bytes 3080 | tf_op jit(solution)/shard_map/ppermute | solution.py:32
  212.6 4.2 %collective-permute-done.33 = f32[1,1,8,8,4,1,1]{2,4,3,6,5,1,0:T(4,128)S(1)} collective-permute-done((f32[1,1,8,8,4,1,1]{2,4,3,6,5,1,0:T(4,128)S(1)}, f32[1,1,8,8,4,1,1]{2,4,3,6,5,1,0:T(4,128)S(1)}, u32[]{:S(2)}, u32[]{:S(2)}) %collective-permute-start.33) | collective-permute-done | bytes 1056 | tf_op jit(solution)/shard_map/ppermute | solution.py:34
  220.4 1.9 collective-permute-start.34
  224.3 4.3 %collective-permute-done.35 = f32[1,1,8,8,4,4,1]{3,2,5,4,6,1,0:T(8,128)S(1)} collective-permute-done((f32[1,1,8,8,4,4,1]{3,2,5,4,6,1,0:T(8,128)S(1)}, f32[1,1,8,8,4,4,1]{3,2,5,4,6,1,0:T(8,128)S(1)}, u32[]{:S(2)}, u32[]{:S(2)}) %collective-permute-start.35) | collective-permute-done | bytes 4128 | tf_op jit(solution)/shard_map/ppermute | solution.py:34
  230.9 40.4 %all-reduce.1 = (f32[]{:T(128)}, f32[]{:T(128)}) all-reduce(f32[]{:T(128)} %get-tuple-element.11, f32[]{:T(128)} %get-tuple-element.10), channel_id=1, replica_groups=mesh['gx'=4,'gy'=2,'gz'=4] {'gx','gy','gz'}, use_global_device_ids=true, to_apply=%region_2.5 | all-reduce | flops 2 | bytes 16 | tf_op jit(solution)/shard_map/psum | solution.py:168
  275.5 1.7 collective-permute-done.37
  277.2 4.8 %collective-permute-start.36 = (f32[1,1,8,8,1,4,1]{2,5,3,6,4,1,0:T(4,128)S(1)}, f32[1,1,8,8,1,4,1]{2,5,3,6,4,1,0:T(4,128)S(1)}, u32[]{:S(2)}, u32[]{:S(2)}) collective-permute-start(f32[1,1,8,8,1,4,1]{2,5,3,6,4,1,0:T(4,128)S(1)} %get-tuple-element.98), channel_id=1, source_target_pairs={{0,8},{8,16},{16,24},{1,9},{9,17},{17,25},{2,10},{10,18},{18,26},{... | collective-permute-start | bytes 3080 | tf_op jit(solution)/shard_map/ppermute | solution.py:32
  285.6 3.0 collective-permute-done.39
  292.2 3.9 %collective-permute-start.40 = (f32[1,1,8,8,4,4,1]{3,2,5,4,6,1,0:T(8,128)S(1)}, f32[1,1,8,8,4,4,1]{3,2,5,4,6,1,0:T(8,128)S(1)}, u32[]{:S(2)}, u32[]{:S(2)}) collective-permute-start(f32[1,1,8,8,4,4,1]{3,2,5,4,6,1,0:T(8,128)S(1)} %bitcast.672), channel_id=1, source_target_pairs={{0,1},{1,2},{2,3},{4,5},{5,6},{6,7},{8,9},{9,10},{10,11},{12,13},{... | collective-permute-start | bytes 12296 | tf_op jit(solution)/shard_map/ppermute | solution.py:32
  298.3 4.0 %collective-permute-done.41 = f32[1,1,8,8,4,4,1]{3,2,5,4,6,1,0:T(8,128)S(1)} collective-permute-done((f32[1,1,8,8,4,4,1]{3,2,5,4,6,1,0:T(8,128)S(1)}, f32[1,1,8,8,4,4,1]{3,2,5,4,6,1,0:T(8,128)S(1)}, u32[]{:S(2)}, u32[]{:S(2)}) %collective-permute-start.41) | collective-permute-done | bytes 4128 | tf_op jit(solution)/shard_map/ppermute | solution.py:34
  304.7 41.1 %all-reduce = (f32[]{:T(128)}, f32[]{:T(128)}) all-reduce(f32[]{:T(128)} %get-tuple-element.9, f32[]{:T(128)} %get-tuple-element.8), channel_id=1, replica_groups=mesh['gx'=4,'gy'=2,'gz'=4] {'gx','gy','gz'}, use_global_device_ids=true, to_apply=%region_6.9 | all-reduce | flops 2 | bytes 16 | tf_op jit(solution)/shard_map/psum | solution.py:168
  (428 shorter events, 109.4 us)
Async XLA Ops:
  7.1 42.3 %copy-start.2 = (f32[8,8,128]{2,0,1:T(8,128)}, f32[8,8,128]{2,0,1:T(8,128)S(1)}, u32[]{:S(2)}) copy-start(f32[8,8,128]{2,0,1:T(8,128)S(1)} %copy.117) | copy-start | bytes 98308
  8.1 41.4 %copy-start.5 = (f32[8,8,128]{2,0,1:T(8,128)}, f32[8,8,128]{2,0,1:T(8,128)S(1)}, u32[]{:S(2)}) copy-start(f32[8,8,128]{2,0,1:T(8,128)S(1)} %copy.109) | copy-start | bytes 98308
  11.1 3.1 collective-permute-start.1
  14.3 6.4 %collective-permute-start = (f32[1,3,8,8,1,4,1]{2,5,3,1,6,4,0:T(4,128)S(1)}, f32[1,3,8,8,1,4,1]{2,5,3,1,6,4,0:T(4,128)S(1)}, u32[]{:S(2)}, u32[]{:S(2)}) collective-permute-start(f32[1,3,8,8,1,4,1]{2,5,3,1,6,4,0:T(4,128)S(1)} %get-tuple-element.41), channel_id=1, source_target_pairs={{0,8},{8,16},{16,24},{1,9},{9,17},{17,25},{2,10},{10,18},{18,26},{... | collective-permute-start | bytes 9224 | tf_op jit(solution)/shard_map/ppermute | solution.py:32
  21.3 6.0 %collective-permute-start.3 = (f32[1,3,8,8,4,1,1]{2,4,3,1,6,5,0:T(4,128)S(1)}, f32[1,3,8,8,4,1,1]{2,4,3,1,6,5,0:T(4,128)S(1)}, u32[]{:S(2)}, u32[]{:S(2)}) collective-permute-start(f32[1,3,8,8,4,1,1]{2,4,3,1,6,5,0:T(4,128)S(1)} %bitcast.645), channel_id=1, source_target_pairs={{4,0},{5,1},{6,2},{7,3},{12,8},{13,9},{14,10},{15,11},{20,16},{21,... | collective-permute-start | bytes 9224 | tf_op jit(solution)/shard_map/ppermute | solution.py:34
  27.4 3.5 copy-start.12
  27.4 3.5 collective-permute-start.2
  31.6 6.7 %collective-permute-start.4 = (f32[1,3,8,8,4,4,1]{3,2,5,4,1,6,0:T(8,128)S(1)}, f32[1,3,8,8,4,4,1]{3,2,5,4,1,6,0:T(8,128)S(1)}, u32[]{:S(2)}, u32[]{:S(2)}) collective-permute-start(f32[1,3,8,8,4,4,1]{3,2,5,4,1,6,0:T(8,128)S(1)} %bitcast.636), channel_id=1, source_target_pairs={{0,1},{1,2},{2,3},{4,5},{5,6},{6,7},{8,9},{9,10},{10,11},{12,13},{... | collective-permute-start | bytes 36872 | tf_op jit(solution)/shard_map/ppermute | solution.py:32
  35.9 7.9 %collective-permute-start.5 = (f32[1,3,8,8,4,4,1]{3,2,5,4,1,6,0:T(8,128)}, f32[1,3,8,8,4,4,1]{3,2,5,4,1,6,0:T(8,128)}, u32[]{:S(2)}, u32[]{:S(2)}) collective-permute-start(f32[1,3,8,8,4,4,1]{3,2,5,4,1,6,0:T(8,128)} %bitcast.638), channel_id=1, source_target_pairs={{1,0},{2,1},{3,2},{5,4},{6,5},{7,6},{9,8},{10,9},{11,10},{13,12},{... | collective-permute-start | bytes 36872 | tf_op jit(solution)/shard_map/ppermute | solution.py:34
  50.0 3.1 collective-permute-start.7
  53.1 6.0 %collective-permute-start.6 = (f32[1,3,8,8,1,4,1]{2,5,3,1,6,4,0:T(4,128)S(1)}, f32[1,3,8,8,1,4,1]{2,5,3,1,6,4,0:T(4,128)S(1)}, u32[]{:S(2)}, u32[]{:S(2)}) collective-permute-start(f32[1,3,8,8,1,4,1]{2,5,3,1,6,4,0:T(4,128)S(1)} %get-tuple-element.35), channel_id=1, source_target_pairs={{0,8},{8,16},{16,24},{1,9},{9,17},{17,25},{2,10},{10,18},{18,26},{... | collective-permute-start | bytes 9224 | tf_op jit(solution)/shard_map/ppermute | solution.py:32
  59.7 6.0 %collective-permute-start.9 = (f32[1,3,8,8,4,1,1]{2,4,3,1,6,5,0:T(4,128)S(1)}, f32[1,3,8,8,4,1,1]{2,4,3,1,6,5,0:T(4,128)S(1)}, u32[]{:S(2)}, u32[]{:S(2)}) collective-permute-start(f32[1,3,8,8,4,1,1]{2,4,3,1,6,5,0:T(4,128)S(1)} %bitcast.647), channel_id=1, source_target_pairs={{4,0},{5,1},{6,2},{7,3},{12,8},{13,9},{14,10},{15,11},{20,16},{21,... | collective-permute-start | bytes 9224 | tf_op jit(solution)/shard_map/ppermute | solution.py:34
  65.8 3.3 collective-permute-start.8
  69.8 6.6 %collective-permute-start.10 = (f32[1,3,8,8,4,4,1]{3,2,5,4,1,6,0:T(8,128)S(1)}, f32[1,3,8,8,4,4,1]{3,2,5,4,1,6,0:T(8,128)S(1)}, u32[]{:S(2)}, u32[]{:S(2)}) collective-permute-start(f32[1,3,8,8,4,4,1]{3,2,5,4,1,6,0:T(8,128)S(1)} %bitcast.639), channel_id=1, source_target_pairs={{0,1},{1,2},{2,3},{4,5},{5,6},{6,7},{8,9},{9,10},{10,11},{12,13},{... | collective-permute-start | bytes 36872 | tf_op jit(solution)/shard_map/ppermute | solution.py:32
  74.1 7.9 %collective-permute-start.11 = (f32[1,3,8,8,4,4,1]{3,2,5,4,1,6,0:T(8,128)}, f32[1,3,8,8,4,4,1]{3,2,5,4,1,6,0:T(8,128)}, u32[]{:S(2)}, u32[]{:S(2)}) collective-permute-start(f32[1,3,8,8,4,4,1]{3,2,5,4,1,6,0:T(8,128)} %bitcast.641), channel_id=1, source_target_pairs={{1,0},{2,1},{3,2},{5,4},{6,5},{7,6},{9,8},{10,9},{11,10},{13,12},{... | collective-permute-start | bytes 36872 | tf_op jit(solution)/shard_map/ppermute | solution.py:34
  88.7 3.3 collective-permute-start.13
  92.8 5.9 %collective-permute-start.12 = (f32[1,3,8,8,1,4,1]{2,5,3,1,6,4,0:T(4,128)S(1)}, f32[1,3,8,8,1,4,1]{2,5,3,1,6,4,0:T(4,128)S(1)}, u32[]{:S(2)}, u32[]{:S(2)}) collective-permute-start(f32[1,3,8,8,1,4,1]{2,5,3,1,6,4,0:T(4,128)S(1)} %get-tuple-element.29), channel_id=1, source_target_pairs={{0,8},{8,16},{16,24},{1,9},{9,17},{17,25},{2,10},{10,18},{18,26},{... | collective-permute-start | bytes 9224 | tf_op jit(solution)/shard_map/ppermute | solution.py:32
  99.4 6.1 %collective-permute-start.15 = (f32[1,3,8,8,4,1,1]{2,4,3,1,6,5,0:T(4,128)S(1)}, f32[1,3,8,8,4,1,1]{2,4,3,1,6,5,0:T(4,128)}, u32[]{:S(2)}, u32[]{:S(2)}) collective-permute-start(f32[1,3,8,8,4,1,1]{2,4,3,1,6,5,0:T(4,128)S(1)} %bitcast.649), channel_id=1, source_target_pairs={{4,0},{5,1},{6,2},{7,3},{12,8},{13,9},{14,10},{15,11},{20,16},{21,... | collective-permute-start | bytes 9224 | tf_op jit(solution)/shard_map/ppermute | solution.py:34
  106.4 3.2 collective-permute-start.14
  110.9 5.8 %copy-start.14 = (f32[8,8,8]{2,1,0:T(8,128)S(1)}, f32[8,8,8]{2,1,0:T(8,128)}, u32[]{:S(2)}) copy-start(f32[8,8,8]{2,1,0:T(8,128)} %constant.133) | copy-start | bytes 6148
  111.7 7.0 %collective-permute-start.16 = (f32[1,3,8,8,4,4,1]{3,2,5,4,1,6,0:T(8,128)}, f32[1,3,8,8,4,4,1]{3,2,5,4,1,6,0:T(8,128)S(1)}, u32[]{:S(2)}, u32[]{:S(2)}) collective-permute-start(f32[1,3,8,8,4,4,1]{3,2,5,4,1,6,0:T(8,128)} %bitcast.76), channel_id=1, source_target_pairs={{0,1},{1,2},{2,3},{4,5},{5,6},{6,7},{8,9},{9,10},{10,11},{12,13},{... | collective-permute-start | bytes 36872 | tf_op jit(solution)/shard_map/ppermute | solution.py:32
  115.2 7.9 %collective-permute-start.17 = (f32[1,3,8,8,4,4,1]{3,2,5,4,1,6,0:T(8,128)}, f32[1,3,8,8,4,4,1]{3,2,5,4,1,6,0:T(8,128)}, u32[]{:S(2)}, u32[]{:S(2)}) collective-permute-start(f32[1,3,8,8,4,4,1]{3,2,5,4,1,6,0:T(8,128)} %bitcast.78), channel_id=1, source_target_pairs={{1,0},{2,1},{3,2},{5,4},{6,5},{7,6},{9,8},{10,9},{11,10},{13,12},{... | collective-permute-start | bytes 36872 | tf_op jit(solution)/shard_map/ppermute | solution.py:34
  133.2 3.5 collective-permute-start.19
  137.5 5.9 %collective-permute-start.18 = (f32[1,3,8,8,1,4,1]{2,5,3,1,6,4,0:T(4,128)S(1)}, f32[1,3,8,8,1,4,1]{2,5,3,1,6,4,0:T(4,128)S(1)}, u32[]{:S(2)}, u32[]{:S(2)}) collective-permute-start(f32[1,3,8,8,1,4,1]{2,5,3,1,6,4,0:T(4,128)S(1)} %get-tuple-element.23), channel_id=1, source_target_pairs={{0,8},{8,16},{16,24},{1,9},{9,17},{17,25},{2,10},{10,18},{18,26},{... | collective-permute-start | bytes 9224 | tf_op jit(solution)/shard_map/ppermute | solution.py:32
  144.1 6.0 %collective-permute-start.21 = (f32[1,3,8,8,4,1,1]{2,4,3,1,6,5,0:T(4,128)S(1)}, f32[1,3,8,8,4,1,1]{2,4,3,1,6,5,0:T(4,128)S(1)}, u32[]{:S(2)}, u32[]{:S(2)}) collective-permute-start(f32[1,3,8,8,4,1,1]{2,4,3,1,6,5,0:T(4,128)S(1)} %bitcast.643), channel_id=1, source_target_pairs={{4,0},{5,1},{6,2},{7,3},{12,8},{13,9},{14,10},{15,11},{20,16},{21,... | collective-permute-start | bytes 9224 | tf_op jit(solution)/shard_map/ppermute | solution.py:34
  150.2 3.5 collective-permute-start.20
  154.3 3.4 copy-start.15
  154.3 3.4 copy-start.16
  154.5 5.4 %collective-permute-start.22 = (f32[1,3,8,8,4,4,1]{3,2,5,4,1,6,0:T(8,128)S(1)}, f32[1,3,8,8,4,4,1]{3,2,5,4,1,6,0:T(8,128)S(1)}, u32[]{:S(2)}, u32[]{:S(2)}) collective-permute-start(f32[1,3,8,8,4,4,1]{3,2,5,4,1,6,0:T(8,128)S(1)} %bitcast.634), channel_id=1, source_target_pairs={{0,1},{1,2},{2,3},{4,5},{5,6},{6,7},{8,9},{9,10},{10,11},{12,13},{... | collective-permute-start | bytes 36872 | tf_op jit(solution)/shard_map/ppermute | solution.py:32
  156.4 7.6 %collective-permute-start.23 = (f32[1,3,8,8,4,4,1]{3,2,5,4,1,6,0:T(8,128)S(1)}, f32[1,3,8,8,4,4,1]{3,2,5,4,1,6,0:T(8,128)S(1)}, u32[]{:S(2)}, u32[]{:S(2)}) collective-permute-start(f32[1,3,8,8,4,4,1]{3,2,5,4,1,6,0:T(8,128)S(1)} %bitcast.632), channel_id=1, source_target_pairs={{1,0},{2,1},{3,2},{5,4},{6,5},{7,6},{9,8},{10,9},{11,10},{13,12},{... | collective-permute-start | bytes 36872 | tf_op jit(solution)/shard_map/ppermute | solution.py:34
  170.0 3.1 collective-permute-start.25
  173.1 5.7 %collective-permute-start.24 = (f32[1,2,8,8,1,4,1]{2,5,3,1,6,4,0:T(4,128)S(1)}, f32[1,2,8,8,1,4,1]{2,5,3,1,6,4,0:T(4,128)S(1)}, u32[]{:S(2)}, u32[]{:S(2)}) collective-permute-start(f32[1,2,8,8,1,4,1]{2,5,3,1,6,4,0:T(4,128)S(1)} %get-tuple-element.55), channel_id=1, source_target_pairs={{0,8},{8,16},{16,24},{1,9},{9,17},{17,25},{2,10},{10,18},{18,26},{... | collective-permute-start | bytes 6152 | tf_op jit(solution)/shard_map/ppermute | solution.py:32
  179.3 5.8 %collective-permute-start.27 = (f32[1,2,8,8,4,1,1]{2,4,3,1,6,5,0:T(4,128)S(1)}, f32[1,2,8,8,4,1,1]{2,4,3,1,6,5,0:T(4,128)S(1)}, u32[]{:S(2)}, u32[]{:S(2)}) collective-permute-start(f32[1,2,8,8,4,1,1]{2,4,3,1,6,5,0:T(4,128)S(1)} %bitcast.656), channel_id=1, source_target_pairs={{4,0},{5,1},{6,2},{7,3},{12,8},{13,9},{14,10},{15,11},{20,16},{21,... | collective-permute-start | bytes 6152 | tf_op jit(solution)/shard_map/ppermute | solution.py:34
  185.2 3.2 collective-permute-start.26
  188.9 4.4 %collective-permute-start.28 = (f32[1,2,8,8,4,4,1]{3,2,5,4,1,6,0:T(8,128)S(1)}, f32[1,2,8,8,4,4,1]{3,2,5,4,1,6,0:T(8,128)S(1)}, u32[]{:S(2)}, u32[]{:S(2)}) collective-permute-start(f32[1,2,8,8,4,4,1]{3,2,5,4,1,6,0:T(8,128)S(1)} %bitcast.658), channel_id=1, source_target_pairs={{0,1},{1,2},{2,3},{4,5},{5,6},{6,7},{8,9},{9,10},{10,11},{12,13},{... | collective-permute-start | bytes 24584 | tf_op jit(solution)/shard_map/ppermute | solution.py:32
  191.0 6.9 %collective-permute-start.29 = (f32[1,2,8,8,4,4,1]{3,2,5,4,1,6,0:T(8,128)S(1)}, f32[1,2,8,8,4,4,1]{3,2,5,4,1,6,0:T(8,128)S(1)}, u32[]{:S(2)}, u32[]{:S(2)}) collective-permute-start(f32[1,2,8,8,4,4,1]{3,2,5,4,1,6,0:T(8,128)S(1)} %bitcast.660), channel_id=1, source_target_pairs={{1,0},{2,1},{3,2},{5,4},{6,5},{7,6},{9,8},{10,9},{11,10},{13,12},{... | collective-permute-start | bytes 24584 | tf_op jit(solution)/shard_map/ppermute | solution.py:34
  202.3 3.1 collective-permute-start.31
  205.4 5.5 %collective-permute-start.30 = (f32[1,1,8,8,1,4,1]{2,5,3,6,4,1,0:T(4,128)S(1)}, f32[1,1,8,8,1,4,1]{2,5,3,6,4,1,0:T(4,128)S(1)}, u32[]{:S(2)}, u32[]{:S(2)}) collective-permute-start(f32[1,1,8,8,1,4,1]{2,5,3,6,4,1,0:T(4,128)S(1)} %get-tuple-element.104), channel_id=1, source_target_pairs={{0,8},{8,16},{16,24},{1,9},{9,17},{17,25},{2,10},{10,18},{18,26},{... | collective-permute-start | bytes 3080 | tf_op jit(solution)/shard_map/ppermute | solution.py:32
  211.2 5.6 %collective-permute-start.33 = (f32[1,1,8,8,4,1,1]{2,4,3,6,5,1,0:T(4,128)S(1)}, f32[1,1,8,8,4,1,1]{2,4,3,6,5,1,0:T(4,128)S(1)}, u32[]{:S(2)}, u32[]{:S(2)}) collective-permute-start(f32[1,1,8,8,4,1,1]{2,4,3,6,5,1,0:T(4,128)S(1)} %bitcast.666), channel_id=1, source_target_pairs={{4,0},{5,1},{6,2},{7,3},{12,8},{13,9},{14,10},{15,11},{20,16},{21,... | collective-permute-start | bytes 3080 | tf_op jit(solution)/shard_map/ppermute | solution.py:34
  216.9 3.1 collective-permute-start.32
  220.4 3.8 %collective-permute-start.34 = (f32[1,1,8,8,4,4,1]{3,2,5,4,6,1,0:T(8,128)S(1)}, f32[1,1,8,8,4,4,1]{3,2,5,4,6,1,0:T(8,128)S(1)}, u32[]{:S(2)}, u32[]{:S(2)}) collective-permute-start(f32[1,1,8,8,4,4,1]{3,2,5,4,6,1,0:T(8,128)S(1)} %bitcast.670), channel_id=1, source_target_pairs={{0,1},{1,2},{2,3},{4,5},{5,6},{6,7},{8,9},{9,10},{10,11},{12,13},{... | collective-permute-start | bytes 12296 | tf_op jit(solution)/shard_map/ppermute | solution.py:32
  222.4 6.2 %collective-permute-start.35 = (f32[1,1,8,8,4,4,1]{3,2,5,4,6,1,0:T(8,128)S(1)}, f32[1,1,8,8,4,4,1]{3,2,5,4,6,1,0:T(8,128)S(1)}, u32[]{:S(2)}, u32[]{:S(2)}) collective-permute-start(f32[1,1,8,8,4,4,1]{3,2,5,4,6,1,0:T(8,128)S(1)} %bitcast.674), channel_id=1, source_target_pairs={{1,0},{2,1},{3,2},{5,4},{6,5},{7,6},{9,8},{10,9},{11,10},{13,12},{... | collective-permute-start | bytes 12296 | tf_op jit(solution)/shard_map/ppermute | solution.py:34
  274.1 3.1 collective-permute-start.37
  277.2 5.4 %collective-permute-start.36 = (f32[1,1,8,8,1,4,1]{2,5,3,6,4,1,0:T(4,128)S(1)}, f32[1,1,8,8,1,4,1]{2,5,3,6,4,1,0:T(4,128)S(1)}, u32[]{:S(2)}, u32[]{:S(2)}) collective-permute-start(f32[1,1,8,8,1,4,1]{2,5,3,6,4,1,0:T(4,128)S(1)} %get-tuple-element.98), channel_id=1, source_target_pairs={{0,8},{8,16},{16,24},{1,9},{9,17},{17,25},{2,10},{10,18},{18,26},{... | collective-permute-start | bytes 3080 | tf_op jit(solution)/shard_map/ppermute | solution.py:32
  282.9 5.6 %collective-permute-start.39 = (f32[1,1,8,8,4,1,1]{2,4,3,6,5,1,0:T(4,128)S(1)}, f32[1,1,8,8,4,1,1]{2,4,3,6,5,1,0:T(4,128)S(1)}, u32[]{:S(2)}, u32[]{:S(2)}) collective-permute-start(f32[1,1,8,8,4,1,1]{2,4,3,6,5,1,0:T(4,128)S(1)} %bitcast.664), channel_id=1, source_target_pairs={{4,0},{5,1},{6,2},{7,3},{12,8},{13,9},{14,10},{15,11},{20,16},{21,... | collective-permute-start | bytes 3080 | tf_op jit(solution)/shard_map/ppermute | solution.py:34
  288.6 3.1 collective-permute-start.38
  292.2 6.0 %collective-permute-start.40 = (f32[1,1,8,8,4,4,1]{3,2,5,4,6,1,0:T(8,128)S(1)}, f32[1,1,8,8,4,4,1]{3,2,5,4,6,1,0:T(8,128)S(1)}, u32[]{:S(2)}, u32[]{:S(2)}) collective-permute-start(f32[1,1,8,8,4,4,1]{3,2,5,4,6,1,0:T(8,128)S(1)} %bitcast.672), channel_id=1, source_target_pairs={{0,1},{1,2},{2,3},{4,5},{5,6},{6,7},{8,9},{9,10},{10,11},{12,13},{... | collective-permute-start | bytes 12296 | tf_op jit(solution)/shard_map/ppermute | solution.py:32
  296.1 6.2 %collective-permute-start.41 = (f32[1,1,8,8,4,4,1]{3,2,5,4,6,1,0:T(8,128)S(1)}, f32[1,1,8,8,4,4,1]{3,2,5,4,6,1,0:T(8,128)S(1)}, u32[]{:S(2)}, u32[]{:S(2)}) collective-permute-start(f32[1,1,8,8,4,4,1]{3,2,5,4,6,1,0:T(8,128)S(1)} %bitcast.668), channel_id=1, source_target_pairs={{1,0},{2,1},{3,2},{5,4},{6,5},{7,6},{9,8},{10,9},{11,10},{13,12},{... | collective-permute-start | bytes 12296 | tf_op jit(solution)/shard_map/ppermute | solution.py:34
  (22 other events, 24.3 us)
where the time goes:
time: 355 us; the launch traced here: 353 us
  starting transfers between devices  93.9 us (26%)
  waiting for transfers between devices  93.5 us (26%)
  blocking collectives  81.5 us (23%)
  local copies, waits for them, and re-layouts  56.4 us (16%)
  other arithmetic  11.6 us (3%)
  between operations  8.86 us (2%)
  matrix products  7.08 us (2%)
    psum x2, blocking collectives, joined_sums(): lax.psum((jnp.sum(residual * precond * inverse_copies), jnp.sum(precond *...  81.5 us
    ppermute x21, waiting for transfers between devices, extended(): lax.ppermute(head, axis, [((i + 1) % count, i) for i in range(ends)])  70.4 us
    ppermute x21, starting transfers between devices, extended(): lax.ppermute(tail, axis, [(i, (i + 1) % count) for i in range(ends)])  66.6 us
    ppermute x21, starting transfers between devices, extended(): lax.ppermute(head, axis, [((i + 1) % count, i) for i in range(ends)])  27.3 us
    ppermute x21, waiting for transfers between devices, extended(): lax.ppermute(tail, axis, [(i, (i + 1) % count) for i in range(ends)])  23.1 us
    dynamic_update_slice x14, local copies, waits for them, and re-layouts, face_write(): return lax.dynamic_update_slice_in_dim(values, flat, node * elements, 3)  22.8 us
  transfers between devices with their start and end apart: 42, of which 41 were waited for; matrix products, arithmetic and copies ran while one was open for 3% of the time, Pallas kernels for 0%

commit v1 on v0

v1 whole, which is shorter than its diff:
```python
import functools

import jax
import jax.numpy as jnp
import numpy as np
from jax import lax
from jax.experimental import pallas as pl
from jax.experimental.pallas import tpu as pltpu
from jax.sharding import PartitionSpec as P

BX = 4
BY = 4
BZ = 1
MESH = pl.DeviceIdType.MESH
AXES = ("gx", "gy", "gz")
ROUNDS = 7

time_step = 0.03
mass_shift = 4.0
inner_nodes = (
    -0.8717401485096066,
    -0.5917001814331423,
    -0.2092992179024789,
    0.2092992179024789,
    0.5917001814331423,
    0.8717401485096066,
)


def legendre_seven(position):
    previous = 1.0
    current_value = position
    for degree_index in range(1, 7):
        following = (
            (2 * degree_index + 1) * position * current_value - degree_index * previous
        ) / (degree_index + 1)
        previous = current_value
        current_value = following
    return current_value


def tables():
    nodes = [-1.0] + list(inner_nodes) + [1.0]
    poly = [legendre_seven(node) for node in nodes]
    weights = np.array([2.0 / (56.0 * value * value) for value in poly])
    derivative = np.zeros((8, 8))
    for i in range(8):
        for j in range(8):
            if i != j:
                derivative[i, j] = poly[i] / (poly[j] * (nodes[i] - nodes[j]))
    derivative[0, 0] = -14.0
    derivative[7, 7] = 14.0
    return weights, derivative.astype(np.float32).astype(np.float64)


def lane_rows(matrix):
    rows = np.zeros((32, 128))
    for t in range(4):
        for u in range(4):
            for h in range(2):
                rows[8 * t + 2 * u, 64 * h : 64 * h + 64] = matrix[2 * t + h, 2 * u + h]
                rows[8 * t + 2 * u + 1, 64 * h : 64 * h + 64] = matrix[2 * t + h, 2 * u + 1 - h]
    return rows


def split_stack(matrix):
    wide = jnp.asarray(matrix, jnp.float32)
    high = np.asarray(matrix, np.float32).astype(jnp.bfloat16)
    low = (np.asarray(matrix, np.float32) - high.astype(np.float32)).astype(jnp.bfloat16)
    del wide
    return np.concatenate([high, high, low], axis=0)


@functools.cache
def constants():
    weights, d = tables()
    eye2, eye8, eye16 = np.eye(2), np.eye(8), np.eye(16)
    forward = np.concatenate(
        [np.kron(np.kron(eye2, d.T), eye8), np.kron(eye16, d.T)], axis=1
    )
    backward = np.concatenate([np.kron(np.kron(eye2, d), eye8), np.kron(eye16, d)], axis=0)
    square = np.kron(np.kron(eye2, d**2), eye8) + np.kron(eye16, d**2)
    quad = np.einsum("a,b,c->abc", weights, weights, weights).reshape(4, 128)
    rows = np.concatenate(
        [lane_rows(d), lane_rows(d.T), lane_rows(d.T**2), quad, np.zeros((4, 128))], axis=0
    )
    return (
        rows.astype(np.float32),
        split_stack(forward),
        split_stack(backward),
        split_stack(square),
    )


def kernel(
    counts,
    vel_ref,
    den_ref,
    place_ref,
    rows_ref,
    fwd_ref,
    bwd_ref,
    sqr_ref,
    adv_ref,
    pre_ref,
    res_ref,
    send_x,
    send_y,
    send_z,
    recv_x,
    recv_y,
    recv_z,
    sums,
    sums_x,
    sums_y,
    sums_z,
    send_sem,
    recv_sem,
    sum_send,
    sum_recv,
):
    f32 = jnp.float32
    me = [lax.axis_index(name) for name in AXES]
    sends = (send_x, send_y, send_z)
    recvs = (recv_x, recv_y, recv_z)
    has = [(me[i] > 0, me[i] < counts[i] - 1) for i in range(3)]

    def at(axis, position):
        return tuple(position if i == axis else me[i] for i in range(3))

    for axis in range(3):
        for side in range(2):

            @pl.when(jnp.logical_not(has[axis][side]))
            def _():
                for r in range(ROUNDS):
                    recvs[axis][r, side] = jnp.zeros(recvs[axis].shape[2:], f32)

    barrier = pltpu.get_barrier_semaphore()
    greeted = 0
    for axis in range(3):
        for k in range(1, counts[axis]):
            pl.semaphore_signal(
                barrier,
                inc=1,
                device_id=at(axis, lax.rem(me[axis] + k, counts[axis])),
                device_id_type=MESH,
            )
            greeted += 1

    lane = lax.broadcasted_iota(jnp.int32, (1, 16, 128), 2)
    row = lax.broadcasted_iota(jnp.int32, (1, 16, 128), 1)
    ex, ey = row // BY, row % BY
    node_b, node_c = (lane // 8) % 8, lane % 8

    r16 = lax.broadcasted_iota(jnp.int32, (16, 16), 0)
    l16 = lax.broadcasted_iota(jnp.int32, (16, 16), 1)
    by_lane = jnp.zeros((16, 16), jnp.int32)
    by_row = jnp.zeros((16, 16), jnp.int32)
    for e in range(16):
        by_lane = jnp.where(l16 == e, place_ref[e], by_lane)
        by_row = jnp.where(r16 == e, place_ref[e], by_row)
    to_place = (by_lane == r16).astype(f32)
    to_slot = (by_row == l16).astype(f32)

    def order(matrix, block):
        return jnp.dot(
            matrix, block, precision=lax.Precision.HIGHEST, preferred_element_type=f32
        )

    placed = [order(to_place, vel_ref[i]) for i in range(3)]
    velocity = [
        jnp.stack([placed[i][:, 128 * t : 128 * t + 128] for i in range(3)]) for t in range(4)
    ]
    dens = order(to_place, den_ref[...])
    quad = [rows_ref[96 + t : 97 + t, :].reshape(1, 1, 128) for t in range(4)]
    mobile = [quad[t] * dens[:, 128 * t : 128 * t + 128].reshape(1, 16, 128) for t in range(4)]

    def half(flag):
        return jnp.where(flag, 0.5, 1.0).astype(f32)

    total = [BX * counts[0], BY * counts[1], BZ * counts[2]]
    pos_x, pos_y = ex + me[0] * BX, ey + me[1] * BY
    share_y = half(
        ((node_b == 0) & (pos_y > 0)) | ((node_b == 7) & (pos_y < total[1] - 1))
    )
    pos_z = row * 0 + me[2]
    share_z = half(((node_c == 0) & (pos_z > 0)) | ((node_c == 7) & (pos_z < total[2] - 1)))
    share_yz = share_y * share_z
    share = [share_yz] * 4
    share[0] = share_yz * half((lane < 64) & (pos_x > 0))
    share[3] = share_yz * half((lane >= 64) & (pos_x < total[0] - 1))

    def along_x(base, v):
        swapped = [pltpu.roll(v[t], 64, 2) for t in range(4)]
        out = []
        for t in range(4):
            acc = None
            for u in range(4):
                k = base + 8 * t + 2 * u
                term = (
                    rows_ref[k : k + 1, :].reshape(1, 1, 128) * v[u]
                    + rows_ref[k + 1 : k + 2, :].reshape(1, 1, 128) * swapped[u]
                )
                acc = term if acc is None else acc + term
            out.append(acc)
        return out

    def split(x):
        high = x.astype(jnp.bfloat16)
        low = (x - high.astype(f32)).astype(jnp.bfloat16)
        return jnp.concatenate([high, low, high], axis=1)

    def along_lanes(v, w_ref):
        c = v[0].shape[0]
        x = jnp.concatenate([v[t].reshape(c * 16, -1) for t in range(4)], axis=0)
        y = jnp.dot(split(x), w_ref[...], preferred_element_type=f32)
        return [y[t * c * 16 : (t + 1) * c * 16].reshape(c, 16, -1) for t in range(4)]

    def copy(r, axis, side, c):
        peer = me[axis] + (1 if side else -1)
        return pltpu.make_async_remote_copy(
            src_ref=sends[axis].at[r, side, pl.ds(0, c)],
            dst_ref=recvs[axis].at[r, 1 - side, pl.ds(0, c)],
            send_sem=send_sem.at[r, axis, side],
            recv_sem=recv_sem.at[r, axis, 1 - side],
            device_id=at(axis, peer),
            device_id_type=MESH,
        )

    def arrival(r, axis, side, c):
        peer = me[axis] + (1 if side else -1)
        return pltpu.make_async_remote_copy(
            src_ref=sends[axis].at[r, side, pl.ds(0, c)],
            dst_ref=recvs[axis].at[r, side, pl.ds(0, c)],
            send_sem=send_sem.at[r, axis, side],
            recv_sem=recv_sem.at[r, axis, side],
            device_id=at(axis, peer),
            device_id_type=MESH,
        )

    def start(r, axis, c):
        for side in range(2):

            @pl.when(has[axis][side])
            def _():
                copy(r, axis, side, c).start()

    def finish(r, axis, c):
        for side in range(2):

            @pl.when(has[axis][side])
            def _():
                arrival(r, axis, side, c).wait_recv()

    def nothing(axis):
        return None

    def assemble(v, r, before=nothing, after=nothing):
        v = list(v)
        c = v[0].shape[0]
        lower, upper = pltpu.roll(v[0], 64, 2), pltpu.roll(v[3], 64, 2)
        send_x[r, 0, :c] = lower[:, 0:8]
        send_x[r, 1, :c] = upper[:, 8:16]
        start(r, 0, c)
        before(0)
        finish(r, 0, c)
        after(0)
        from_low = jnp.concatenate([upper[:, 0:8], recv_x[r, 0, :c]], axis=1)
        from_high = jnp.concatenate([recv_x[r, 1, :c], lower[:, 8:16]], axis=1)
        d_low = pltpu.roll(jnp.where(row < 12, upper, from_low), 4, 1)
        d_high = pltpu.roll(jnp.where(row >= 4, lower, from_high), 12, 1)
        v[0] = v[0] + jnp.where(lane < 64, d_low, 0.0)
        v[3] = v[3] + jnp.where(lane >= 64, d_high, 0.0)
        lower = v[0]
        upper = pltpu.roll(v[0], 72, 2)
        for t in range(1, 4):
            lower = jnp.where(node_b == t, pltpu.roll(v[t], 8 * t, 2), lower)
            upper = jnp.where(node_b == t, pltpu.roll(v[t], 72 + 8 * t, 2), upper)
        send_y[r, 0, :c] = lower
        send_y[r, 1, :c] = upper
        start(r, 1, c)
        before(1)
        in_low, in_high = pltpu.roll(upper, 1, 1), pltpu.roll(lower, 15, 1)
        finish(r, 1, c)
        after(1)
        d_low = jnp.where(ey > 0, in_low, pltpu.roll(recv_y[r, 0, :c], 13, 1))
        d_high = jnp.where(ey < 3, in_high, pltpu.roll(recv_y[r, 1, :c], 3, 1))
        for t in range(4):
            low = d_low if t == 0 else pltpu.roll(d_low, 128 - 8 * t, 2)
            high = pltpu.roll(d_high, 56 - 8 * t, 2)
            v[t] = v[t] + jnp.where(node_b == 0, low, jnp.where(node_b == 7, high, 0.0))
        lower = v[0]
        upper = pltpu.roll(v[0], 121, 2)
        for t in range(1, 4):
            lower = jnp.where(node_c == t, pltpu.roll(v[t], t, 2), lower)
            upper = jnp.where(node_c == t, pltpu.roll(v[t], 121 + t, 2), upper)
        send_z[r, 0, :c] = lower
        send_z[r, 1, :c] = upper
        start(r, 2, c)
        before(2)
        finish(r, 2, c)
        after(2)
        d_low, d_high = recv_z[r, 0, :c], recv_z[r, 1, :c]
        for t in range(4):
            low = d_low if t == 0 else pltpu.roll(d_low, 128 - t, 2)
            high = pltpu.roll(d_high, 7 - t, 2)
            v[t] = v[t] + jnp.where(node_c == 0, low, jnp.where(node_c == 7, high, 0.0))
        return v

    def advect(v):
        dx = along_x(0, v)
        dyz = along_lanes(v, fwd_ref)
        return [
            velocity[t][0:1] * dx[t]
            + velocity[t][1:2] * dyz[t][:, :, :128]
            + velocity[t][2:3] * dyz[t][:, :, 128:]
            for t in range(4)
        ]

    first = advect(velocity)
    square_x = along_x(64, mobile)
    square_yz = along_lanes(mobile, sqr_ref)
    diag = [mass_shift * quad[t] + square_x[t] + square_yz[t] for t in range(4)]
    pl.semaphore_wait(barrier, greeted)
    joint = assemble([jnp.concatenate([first[t], diag[t]], axis=0) for t in range(4)], 0)
    inverse_jacobi = [1.0 / joint[t][3:4] for t in range(4)]
    k1 = [joint[t][0:3] * share[t] for t in range(4)]
    total_rate = k1
    v = [velocity[t] - (0.5 * time_step) * k1[t] for t in range(4)]
    for r, step, weight in ((1, 0.5, 2.0), (2, 1.0, 2.0), (3, 0.0, 1.0)):
        g = assemble(advect(v), r)
        g = [g[t] * share[t] for t in range(4)]
        total_rate = [total_rate[t] + weight * g[t] for t in range(4)]
        if step:
            v = [velocity[t] - (step * time_step) * g[t] for t in range(4)]
    advected = [velocity[t] - (time_step / 6.0) * total_rate[t] for t in range(4)]

    dx = along_x(0, [advected[t][0:1] for t in range(4)])
    dyz = along_lanes([advected[t][1:3] for t in range(4)], fwd_ref)
    div = [dx[t] + dyz[t][0:1, :, :128] + dyz[t][1:2, :, 128:] for t in range(4)]
    source = assemble(div, 4)
    r0 = [source[t] * (quad[t] * (-1.0 / time_step)) for t in range(4)]

    def local(v):
        dx = along_x(0, v)
        dyz = along_lanes(v, fwd_ref)
        gx = [mobile[t] * dx[t] for t in range(4)]
        gyz = [
            jnp.concatenate(
                [mobile[t] * dyz[t][:, :, :128], mobile[t] * dyz[t][:, :, 128:]], axis=2
            )
            for t in range(4)
        ]
        bx = along_x(32, gx)
        byz = along_lanes(gyz, bwd_ref)
        return [(mass_shift * quad[t]) * v[t] + bx[t] + byz[t] for t in range(4)]

    def dot_row(a, b, scale=None):
        acc = None
        for t in range(4):
            term = a[t] * b[t]
            if scale is not None:
                term = term * scale[t]
            acc = term if acc is None else acc + term
        return jnp.sum(acc[0], axis=0, keepdims=True)

    z0 = [r0[t] * inverse_jacobi[t] for t in range(4)]
    lz = local(z0)
    rho_row = dot_row(r0, z0, share)
    gamma_row = dot_row(z0, lz)
    s = assemble(lz, 5)
    w = [s[t] * inverse_jacobi[t] for t in range(4)]
    lw = local(w)
    delta_row = dot_row(s, w, share)
    eps_row = dot_row(w, lw)
    sums[0] = jnp.concatenate(
        [rho_row, gamma_row, delta_row, eps_row, jnp.zeros((4, 128), f32)], axis=0
    )
    sum_bufs = (sums_x, sums_y, sums_z)

    def sum_copy(axis, k):
        return pltpu.make_async_remote_copy(
            src_ref=sums.at[axis],
            dst_ref=sum_bufs[axis].at[k - 1],
            send_sem=sum_send[axis].at[k - 1],
            recv_sem=sum_recv[axis].at[k - 1],
            device_id=at(axis, lax.rem(me[axis] + k, counts[axis])),
            device_id_type=MESH,
        )

    def sum_start(axis):
        for k in range(1, counts[axis]):
            sum_copy(axis, k).start()

    def sum_finish(axis):
        joined = sums[axis]
        for k in range(1, counts[axis]):
            sum_copy(axis, k).wait_recv()
            joined = joined + sum_bufs[axis][k - 1]
        sums[axis + 1] = joined

    t_vec = assemble(lw, 6, sum_start, sum_finish)
    four = jnp.sum(sums[3], axis=1, keepdims=True)
    rho, gamma, delta, eps = (four[i : i + 1].reshape(1, 1, 1) for i in range(4))
    alpha0 = rho / gamma
    rho1 = rho - 2.0 * alpha0 * gamma + alpha0 * alpha0 * delta
    beta = rho1 / rho
    cross = gamma - alpha0 * delta
    curve = gamma - 2.0 * alpha0 * delta + alpha0 * alpha0 * eps
    curve = curve + 2.0 * beta * cross + beta * beta * gamma
    alpha1 = rho1 / curve
    along = alpha0 + alpha1 * (1.0 + beta)
    side_step = alpha0 * alpha1

    def put(field):
        return order(to_slot, field)

    for i in range(3):
        adv_ref[i] = put(jnp.concatenate([advected[t][i] for t in range(4)], axis=1))
    pre_ref[...] = put(
        jnp.concatenate([(along * z0[t] - side_step * w[t])[0] for t in range(4)], axis=1)
    )
    res_ref[...] = put(
        jnp.concatenate(
            [(r0[t] - along * s[t] + side_step * t_vec[t])[0] for t in range(4)], axis=1
        )
    )
    for r in range(ROUNDS):
        c = 4 if r == 0 else 3 if r < 4 else 1
        for axis in range(3):
            for side in range(2):

                @pl.when(has[axis][side])
                def _():
                    copy(r, axis, side, c).wait_send()

    for axis in range(3):
        for k in range(1, counts[axis]):
            sum_copy(axis, k).wait_send()


def per_device(counts, velocity, inv_density, element_place):
    f32 = jnp.float32
    rows, forward, backward, square = constants()
    elements = element_place.shape[0]
    points = inv_density.shape[0]
    vmem = pl.BlockSpec(memory_space=pltpu.VMEM)
    faces_x = pltpu.VMEM((ROUNDS, 2, 4, 8, 128), f32)
    faces = pltpu.VMEM((ROUNDS, 2, 4, 16, 128), f32)
    dma = pltpu.SemaphoreType.DMA
    peers = [n - 1 for n in counts]
    advected, pressure, residual = pl.pallas_call(
        functools.partial(kernel, counts),
        out_shape=(
            jax.ShapeDtypeStruct((3, elements, points), f32),
            jax.ShapeDtypeStruct((elements, points), f32),
            jax.ShapeDtypeStruct((elements, points), f32),
        ),
        in_specs=[vmem, vmem, pl.BlockSpec(memory_space=pltpu.SMEM), vmem, vmem, vmem, vmem],
        out_specs=(vmem, vmem, vmem),
        scratch_shapes=[
            faces_x,
            faces,
            faces,
            faces_x,
            faces,
            faces,
            pltpu.VMEM((4, 8, 128), f32),
            pltpu.VMEM((peers[0], 8, 128), f32),
            pltpu.VMEM((peers[1], 8, 128), f32),
            pltpu.VMEM((peers[2], 8, 128), f32),
            dma((ROUNDS, 3, 2)),
            dma((ROUNDS, 3, 2)),
            [dma((n,)) for n in peers],
            [dma((n,)) for n in peers],
        ],
        compiler_params=pltpu.CompilerParams(collective_id=0, has_side_effects=True),
    )(
        velocity.transpose(0, 2, 1),
        inv_density.T,
        element_place,
        jnp.asarray(rows),
        jnp.asarray(forward),
        jnp.asarray(backward),
        jnp.asarray(square),
    )
    return advected.transpose(0, 2, 1), pressure.T, residual.T


def solution(mesh):
    counts = tuple(mesh.shape[name] for name in AXES)
    placed = (P(None, None, AXES), P(None, AXES), P(AXES))
    return jax.shard_map(
        functools.partial(per_device, counts),
        mesh=mesh,
        in_specs=placed,
        out_specs=(P(None, None, AXES), P(None, AXES), P(None, AXES)),
        check_vma=False,
    )
```

time: 355 us -> 67.7 us (0.19)
  starting transfers between devices: 93.9 us -> 0 us
  waiting for transfers between devices: 93.5 us -> 0 us
  blocking collectives: 81.5 us -> 0 us
  Pallas kernels: 0 us -> 63.8 us
  local copies, waits for them, and re-layouts: 56.4 us -> 2.93 us
  other arithmetic: 11.6 us -> 0 us
  between operations: 8.86 us -> 0.65 us
  matrix products: 7.08 us -> 0 us
    ppermute x42 -> x0, starting transfers between devices: 93.9 us -> none  [the longest x21 66.6 us: extended(): lax.ppermute(tail, axis, [(i, (i + 1) % count) for i in range(ends)])]
    ppermute x42 -> x0, waiting for transfers between devices: 93.5 us -> none  [the longest x21 70.4 us: extended(): lax.ppermute(head, axis, [((i + 1) % count, i) for i in range(ends)])]
    psum x2 -> x0, blocking collectives: 81.5 us -> none  [joined_sums(): lax.psum((jnp.sum(residual * precond * inverse_copies), jnp.sum(precond *...]
    pallas_call x0 -> x1, Pallas kernels: none -> 63.8 us  [per_device(): pl.pallas_call(functools.partial(kernel, counts), out_shape=(jax.ShapeDty...]
    dynamic_update_slice x42 -> x0, local copies, waits for them, and re-layouts: 23.7 us -> none  [the longest x14 22.8 us: face_write(): return lax.dynamic_update_slice_in_dim(values, flat, node * elements, 3)]
    slice x73 -> x0, local copies, waits for them, and re-layouts: 9.05 us -> none  [the longest x21 5.12 us: face_take(): lax.slice_in_dim(values, node * elements, (node + 1) * elements, axis=3)]
    dot_general x30 -> x0, matrix products: 7.08 us -> none  [the longest x10 2.63 us: apply_along(): jnp.einsum('ij,sjbk->sibk', matrix, values, precision=lax.Precision.HIGHEST)]
    add x56 -> x0, other arithmetic: 6.1 us -> none  [the longest x21 5.05 us: assemble_axis(): last_sum = upper_edge + arrived[3]]
  transfers between devices with their start and end apart: 42 -> 0, of which waited for: 41 -> 0; matrix products, arithmetic and copies ran while one was open for 3% -> 0% of each run, Pallas kernels for 0% -> 0%
where the time goes in v1:
time: 67.7 us; the launch traced here: 67.4 us
  Pallas kernels  63.8 us (94%)
  local copies, waits for them, and re-layouts  2.93 us (4%)
    pallas_call x1, Pallas kernels, per_device(): pl.pallas_call(functools.partial(kernel, counts), out_shape=(jax.ShapeDty...  63.8 us
    unnamed x7, local copies, waits for them, and re-layouts  2.93 us

profile of v1, /device:TPU:0, one launch (start us, length us, event | category | flops | bytes accessed | tf_op | source)
XLA Modules:
  0.0 67.4 jit_solution(18194955833073651219)
XLA Ops:
  0.6 63.8 %shard_map.94 = (f32[3,16,512]{2,1,0:T(8,128)}, f32[16,512]{1,0:T(8,128)}, f32[16,512]{1,0:T(8,128)}) custom-call(f32[3,16,512]{2,1,0:T(8,128)} %bitcast.5, f32[16,512]{1,0:T(8,128)} %bitcast.7, s32[16]{0:T(128)} %place_ref.1, f32[104,128]{1,0:T(8,128)} %constant.8.clone.rows_ref, bf16[384,256]{1,0:T(8,128)(2,1)} %constant.9.clone.fwd_ref, ...), custom_call_target="tpu_custom_call" | custom-call | tf_op jit(solution)/shard_map/pallas_call | solution.py:453
  64.5 0.0 copy-start.1
  64.5 1.5 %copy.13 = f32[3,512,16]{1,2,0:T(8,128)} copy(f32[3,512,16]{1,2,0:T(8,128)} %bitcast.6) | data formatting | bytes 196608
  66.0 0.0 copy-done.1
  66.0 0.0 copy-start
  66.0 0.6 copy.14
  66.6 0.2 copy-done
  66.8 0.6 copy.15
Async XLA Ops:
  64.5 1.6 %copy-start.1 = (f32[16,512]{1,0:T(8,128)S(1)}, f32[16,512]{1,0:T(8,128)}, u32[]{:S(2)}) copy-start(f32[16,512]{1,0:T(8,128)} %get-tuple-element.7) | copy-start | bytes 98308
  66.0 0.8 %copy-start = (f32[16,512]{1,0:T(8,128)S(1)}, f32[16,512]{1,0:T(8,128)}, u32[]{:S(2)}) copy-start(f32[16,512]{1,0:T(8,128)} %get-tuple-element.8) | copy-start | bytes 98308

commit v2 on v1

--- a/solution.py
+++ b/solution.py
@@ -64,10 +64,8 @@
 
 
 def split_stack(matrix):
-    wide = jnp.asarray(matrix, jnp.float32)
     high = np.asarray(matrix, np.float32).astype(jnp.bfloat16)
     low = (np.asarray(matrix, np.float32) - high.astype(np.float32)).astype(jnp.bfloat16)
-    del wide
     return np.concatenate([high, high, low], axis=0)
 
 
@@ -107,8 +105,7 @@
     send_x,
     send_y,
     send_z,
-    recv_x,
-    recv_y,
+    recv_xy,
     recv_z,
     sums,
     sums_x,
@@ -121,32 +118,10 @@
 ):
     f32 = jnp.float32
     me = [lax.axis_index(name) for name in AXES]
-    sends = (send_x, send_y, send_z)
-    recvs = (recv_x, recv_y, recv_z)
     has = [(me[i] > 0, me[i] < counts[i] - 1) for i in range(3)]
 
     def at(axis, position):
         return tuple(position if i == axis else me[i] for i in range(3))
-
-    for axis in range(3):
-        for side in range(2):
-
-            @pl.when(jnp.logical_not(has[axis][side]))
-            def _():
-                for r in range(ROUNDS):
-                    recvs[axis][r, side] = jnp.zeros(recvs[axis].shape[2:], f32)
-
-    barrier = pltpu.get_barrier_semaphore()
-    greeted = 0
-    for axis in range(3):
-        for k in range(1, counts[axis]):
-            pl.semaphore_signal(
-                barrier,
-                inc=1,
-                device_id=at(axis, lax.rem(me[axis] + k, counts[axis])),
-                device_id_type=MESH,
-            )
-            greeted += 1
 
     lane = lax.broadcasted_iota(jnp.int32, (1, 16, 128), 2)
     row = lax.broadcasted_iota(jnp.int32, (1, 16, 128), 1)
@@ -217,94 +192,201 @@
         y = jnp.dot(split(x), w_ref[...], preferred_element_type=f32)
         return [y[t * c * 16 : (t + 1) * c * 16].reshape(c, 16, -1) for t in range(4)]
 
-    def copy(r, axis, side, c):
-        peer = me[axis] + (1 if side else -1)
+    directions = [
+        (dx, dy, dz)
+        for dx in (-1, 1, 0)
+        for dy in (0, -1, 1)
+        for dz in (0, -1, 1)
+        if (dx, dy, dz) != (0, 0, 0)
+    ]
+
+    def code(d):
+        return (d[0] + 1) * 9 + (d[1] + 1) * 3 + d[2] + 1
+
+    def exists(d):
+        flag = None
+        for i in range(3):
+            if d[i]:
+                here = has[i][1 if d[i] > 0 else 0]
+                flag = here if flag is None else jnp.logical_and(flag, here)
+        return flag
+
+    def side_of(step):
+        return 1 if step > 0 else 0
+
+    def source(r, d, c):
+        if d[0]:
+            return send_x.at[r, side_of(d[0])]
+        if d[1]:
+            return send_y.at[r, side_of(d[1])]
+        return send_z.at[r, side_of(d[2]), pl.ds(0, c)]
+
+    def target(r, d, c):
+        if d[0] or d[1]:
+            return recv_xy.at[r, code(d)]
+        return recv_z.at[r, side_of(d[2]), pl.ds(0, c)]
+
+    def copy(r, d, c, incoming):
+        back = d if incoming else tuple(-i for i in d)
         return pltpu.make_async_remote_copy(
-            src_ref=sends[axis].at[r, side, pl.ds(0, c)],
-            dst_ref=recvs[axis].at[r, 1 - side, pl.ds(0, c)],
-            send_sem=send_sem.at[r, axis, side],
-            recv_sem=recv_sem.at[r, axis, 1 - side],
-            device_id=at(axis, peer),
+            src_ref=source(r, d, c),
+            dst_ref=target(r, back, c),
+            send_sem=send_sem.at[r, code(d)],
+            recv_sem=recv_sem.at[r, code(back)],
+            device_id=tuple(me[i] + d[i] for i in range(3)),
             device_id_type=MESH,
         )
 
-    def arrival(r, axis, side, c):
-        peer = me[axis] + (1 if side else -1)
-        return pltpu.make_async_remote_copy(
-            src_ref=sends[axis].at[r, side, pl.ds(0, c)],
-            dst_ref=recvs[axis].at[r, side, pl.ds(0, c)],
-            send_sem=send_sem.at[r, axis, side],
-            recv_sem=recv_sem.at[r, axis, side],
-            device_id=at(axis, peer),
-            device_id_type=MESH,
-        )
-
-    def start(r, axis, c):
-        for side in range(2):
-
-            @pl.when(has[axis][side])
+    def start(r, c, chosen):
+        for d in chosen:
+
+            @pl.when(exists(d))
             def _():
-                copy(r, axis, side, c).start()
-
-    def finish(r, axis, c):
-        for side in range(2):
-
-            @pl.when(has[axis][side])
+                copy(r, d, c, False).start()
+
+    def finish(r, c):
+        for d in directions:
+
+            @pl.when(exists(d))
             def _():
-                arrival(r, axis, side, c).wait_recv()
-
-    def nothing(axis):
+                copy(r, d, c, True).wait_recv()
+
+    barrier = pltpu.get_barrier_semaphore()
+    for d in directions:
+
+        @pl.when(exists(d))
+        def _():
+            pl.semaphore_signal(
+                barrier,
+                inc=1,
+                device_id=tuple(me[i] + d[i] for i in range(3)),
+                device_id_type=MESH,
+            )
+
+    for axis in range(3):
+        for k in range(1, counts[axis]):
+            pl.semaphore_signal(
+                barrier,
+                inc=1,
+                device_id=at(axis, lax.rem(me[axis] + k, counts[axis])),
+                device_id_type=MESH,
+            )
+    near = [1 + (me[i] > 0).astype(jnp.int32) + (me[i] < counts[i] - 1).astype(jnp.int32) for i in range(3)]
+    greeted = near[0] * near[1] * near[2] - 1 + sum(n - 1 for n in counts)
+    for d in directions:
+
+        @pl.when(jnp.logical_not(exists(d)))
+        def _():
+            for r in range(ROUNDS):
+                if d[0] or d[1]:
+                    recv_xy[r, code(d)] = jnp.zeros((8, 128), f32)
+                else:
+                    recv_z[r, side_of(d[2])] = jnp.zeros((4, 8, 128), f32)
+
+    sub8 = lax.broadcasted_iota(jnp.int32, (8, 128), 0)
+    lane8 = lax.broadcasted_iota(jnp.int32, (8, 128), 1)
+    quarter = sub8 // 4 + 2 * (lane8 // 64)
+    b8, c8, y8 = (lane8 // 8) % 8, lane8 % 8, sub8 % 4
+
+    def turn(x, shift, axis):
+        size = x.shape[axis]
+        shift = shift % size
+        return pltpu.roll(x, shift, axis) if shift else x
+
+    def requarter(x, k, base):
+        if (k ^ base) & 1:
+            x = turn(x, 4, 0)
+        if (k ^ base) & 2:
+            x = turn(x, 64, 1)
+        return x
+
+    def nothing():
         return None
 
-    def assemble(v, r, before=nothing, after=nothing):
+    def z_joined(r, dx, dy):
+        mid = recv_xy[r, code((dx, dy, 0))]
+        low = turn(recv_xy[r, code((dx, dy, -1))], -7, 1)
+        high = turn(recv_xy[r, code((dx, dy, 1))], 7, 1)
+        return mid + jnp.where(c8 == 0, low, jnp.where(c8 == 7, high, 0.0))
+
+    def assemble(v, r, between=nothing):
         v = list(v)
         c = v[0].shape[0]
-        lower, upper = pltpu.roll(v[0], 64, 2), pltpu.roll(v[3], 64, 2)
-        send_x[r, 0, :c] = lower[:, 0:8]
-        send_x[r, 1, :c] = upper[:, 8:16]
-        start(r, 0, c)
-        before(0)
-        finish(r, 0, c)
-        after(0)
-        from_low = jnp.concatenate([upper[:, 0:8], recv_x[r, 0, :c]], axis=1)
-        from_high = jnp.concatenate([recv_x[r, 1, :c], lower[:, 8:16]], axis=1)
-        d_low = pltpu.roll(jnp.where(row < 12, upper, from_low), 4, 1)
-        d_high = pltpu.roll(jnp.where(row >= 4, lower, from_high), 12, 1)
-        v[0] = v[0] + jnp.where(lane < 64, d_low, 0.0)
-        v[3] = v[3] + jnp.where(lane >= 64, d_high, 0.0)
+        lower, upper = turn(v[0], 64, 2), turn(v[3], 64, 2)
+        v[0] = v[0] + jnp.where((lane < 64) & (row >= 4), turn(upper, 4, 1), 0.0)
+        v[3] = v[3] + jnp.where((lane >= 64) & (row < 12), turn(lower, -4, 1), 0.0)
         lower = v[0]
-        upper = pltpu.roll(v[0], 72, 2)
+        upper = turn(v[0], 72, 2)
         for t in range(1, 4):
-            lower = jnp.where(node_b == t, pltpu.roll(v[t], 8 * t, 2), lower)
-            upper = jnp.where(node_b == t, pltpu.roll(v[t], 72 + 8 * t, 2), upper)
-        send_y[r, 0, :c] = lower
-        send_y[r, 1, :c] = upper
-        start(r, 1, c)
-        before(1)
-        in_low, in_high = pltpu.roll(upper, 1, 1), pltpu.roll(lower, 15, 1)
-        finish(r, 1, c)
-        after(1)
-        d_low = jnp.where(ey > 0, in_low, pltpu.roll(recv_y[r, 0, :c], 13, 1))
-        d_high = jnp.where(ey < 3, in_high, pltpu.roll(recv_y[r, 1, :c], 3, 1))
+            lower = jnp.where(node_b == t, turn(v[t], 8 * t, 2), lower)
+            upper = jnp.where(node_b == t, turn(v[t], 72 + 8 * t, 2), upper)
+        d_low = jnp.where(ey > 0, turn(upper, 1, 1), 0.0)
+        d_high = jnp.where(ey < 3, turn(lower, -1, 1), 0.0)
+
+        def add_y(d_low, d_high):
+            for t in range(4):
+                low, high = turn(d_low, -8 * t, 2), turn(d_high, 56 - 8 * t, 2)
+                v[t] = v[t] + jnp.where(node_b == 0, low, jnp.where(node_b == 7, high, 0.0))
+
+        add_y(d_low, d_high)
+        lower, upper = lower + d_low, upper + d_high
+        for side in range(2):
+            base = 3 * side
+            acc = None
+            for k in range(c):
+                part = requarter(v[3 * side][k, 8 * side : 8 * side + 8], k, base)
+                acc = part if acc is None else jnp.where(quarter == k, part, acc)
+            send_x[r, side] = acc
+        start(r, c, [d for d in directions if d[0]])
+        for side, face in ((0, lower), (1, upper)):
+            acc = None
+            for k in range(c):
+                part = jnp.where(b8 < 4, face[k, 0:8], turn(face[k, 8:16], 32, 1))
+                part = turn(part, k + 5 * side, 0)
+                acc = part if acc is None else jnp.where(y8 == k, part, acc)
+            send_y[r, side] = acc
+        start(r, c, [d for d in directions if not d[0] and d[1]])
+        lower = v[0]
+        upper = turn(v[0], -7, 2)
+        for t in range(1, 4):
+            lower = jnp.where(node_c == t, turn(v[t], t, 2), lower)
+            upper = jnp.where(node_c == t, turn(v[t], t - 7, 2), upper)
+        for side, face in ((0, lower), (1, upper)):
+            for k in range(c):
+                send_z[r, side, k] = jnp.where(c8 < 4, face[k, 0:8], turn(face[k, 8:16], 4, 1))
+        start(r, c, [d for d in directions if not d[0] and not d[1]])
+        between()
+        finish(r, c)
+        for side in range(2):
+            dx = 2 * side - 1
+            low = turn(turn(z_joined(r, dx, -1), -56, 1), -3, 0)
+            high = turn(turn(z_joined(r, dx, 1), 56, 1), 3, 0)
+            face = z_joined(r, dx, 0) + jnp.where(
+                (y8 == 0) & (b8 == 0), low, jnp.where((y8 == 3) & (b8 == 7), high, 0.0)
+            )
+            base = 3 * side
+            parts = [
+                jnp.where(quarter == base, requarter(face, k, base), 0.0) for k in range(c)
+            ]
+            part = jnp.stack(parts)
+            zero = jnp.zeros_like(part)
+            pair = [part, zero] if side == 0 else [zero, part]
+            v[3 * side] = v[3 * side] + jnp.concatenate(pair, axis=1)
+        got = []
+        for side in range(2):
+            face = z_joined(r, 0, 2 * side - 1)
+            parts = []
+            for k in range(c):
+                part = jnp.where(y8 == 3 * side, turn(face, 3 * side - k, 0), 0.0)
+                parts.append(jnp.concatenate([part, turn(part, -32, 1)], axis=0))
+            got.append(jnp.stack(parts))
+        add_y(got[0], got[1])
+        got = []
+        for side in range(2):
+            face = recv_z[r, side, :c]
+            got.append(jnp.concatenate([face, turn(face, -4, 2)], axis=1))
         for t in range(4):
-            low = d_low if t == 0 else pltpu.roll(d_low, 128 - 8 * t, 2)
-            high = pltpu.roll(d_high, 56 - 8 * t, 2)
-            v[t] = v[t] + jnp.where(node_b == 0, low, jnp.where(node_b == 7, high, 0.0))
-        lower = v[0]
-        upper = pltpu.roll(v[0], 121, 2)
-        for t in range(1, 4):
-            lower = jnp.where(node_c == t, pltpu.roll(v[t], t, 2), lower)
-            upper = jnp.where(node_c == t, pltpu.roll(v[t], 121 + t, 2), upper)
-        send_z[r, 0, :c] = lower
-        send_z[r, 1, :c] = upper
-        start(r, 2, c)
-        before(2)
-        finish(r, 2, c)
-        after(2)
-        d_low, d_high = recv_z[r, 0, :c], recv_z[r, 1, :c]
-        for t in range(4):
-            low = d_low if t == 0 else pltpu.roll(d_low, 128 - t, 2)
-            high = pltpu.roll(d_high, 7 - t, 2)
+            low, high = turn(got[0], -t, 2), turn(got[1], 7 - t, 2)
             v[t] = v[t] + jnp.where(node_c == 0, low, jnp.where(node_c == 7, high, 0.0))
         return v
 
@@ -339,8 +421,8 @@
     dx = along_x(0, [advected[t][0:1] for t in range(4)])
     dyz = along_lanes([advected[t][1:3] for t in range(4)], fwd_ref)
     div = [dx[t] + dyz[t][0:1, :, :128] + dyz[t][1:2, :, 128:] for t in range(4)]
-    source = assemble(div, 4)
-    r0 = [source[t] * (quad[t] * (-1.0 / time_step)) for t in range(4)]
+    total_div = assemble(div, 4)
+    r0 = [total_div[t] * (quad[t] * (-1.0 / time_step)) for t in range(4)]
 
     def local(v):
         dx = along_x(0, v)
@@ -400,7 +482,12 @@
             joined = joined + sum_bufs[axis][k - 1]
         sums[axis + 1] = joined
 
-    t_vec = assemble(lw, 6, sum_start, sum_finish)
+    def reduce_sums():
+        for axis in range(3):
+            sum_start(axis)
+            sum_finish(axis)
+
+    t_vec = assemble(lw, 6, reduce_sums)
     four = jnp.sum(sums[3], axis=1, keepdims=True)
     rho, gamma, delta, eps = (four[i : i + 1].reshape(1, 1, 1) for i in range(4))
     alpha0 = rho / gamma
@@ -428,12 +515,11 @@
     )
     for r in range(ROUNDS):
         c = 4 if r == 0 else 3 if r < 4 else 1
-        for axis in range(3):
-            for side in range(2):
-
-                @pl.when(has[axis][side])
-                def _():
-                    copy(r, axis, side, c).wait_send()
+        for d in directions:
+
+            @pl.when(exists(d))
+            def _():
+                copy(r, d, c, False).wait_send()
 
     for axis in range(3):
         for k in range(1, counts[axis]):
@@ -446,8 +532,8 @@
     elements = element_place.shape[0]
     points = inv_density.shape[0]
     vmem = pl.BlockSpec(memory_space=pltpu.VMEM)
-    faces_x = pltpu.VMEM((ROUNDS, 2, 4, 8, 128), f32)
-    faces = pltpu.VMEM((ROUNDS, 2, 4, 16, 128), f32)
+    faces = pltpu.VMEM((ROUNDS, 2, 8, 128), f32)
+    faces_z = pltpu.VMEM((ROUNDS, 2, 4, 8, 128), f32)
     dma = pltpu.SemaphoreType.DMA
     peers = [n - 1 for n in counts]
     advected, pressure, residual = pl.pallas_call(
@@ -460,18 +546,17 @@
         in_specs=[vmem, vmem, pl.BlockSpec(memory_space=pltpu.SMEM), vmem, vmem, vmem, vmem],
         out_specs=(vmem, vmem, vmem),
         scratch_shapes=[
-            faces_x,
             faces,
             faces,
-            faces_x,
-            faces,
-            faces,
+            faces_z,
+            pltpu.VMEM((ROUNDS, 27, 8, 128), f32),
+            faces_z,
             pltpu.VMEM((4, 8, 128), f32),
             pltpu.VMEM((peers[0], 8, 128), f32),
             pltpu.VMEM((peers[1], 8, 128), f32),
             pltpu.VMEM((peers[2], 8, 128), f32),
-            dma((ROUNDS, 3, 2)),
-            dma((ROUNDS, 3, 2)),
+            dma((ROUNDS, 27)),
+            dma((ROUNDS, 27)),
             [dma((n,)) for n in peers],
             [dma((n,)) for n in peers],
         ],

time: 67.7 us -> 49.5 us (0.73)
  Pallas kernels: 63.8 us -> 45.7 us
    pallas_call x1, Pallas kernels: 63.8 us -> 45.7 us  [per_device(): pl.pallas_call(functools.partial(kernel, counts), out_shape=(jax.ShapeDty...]
where the time goes in v2:
time: 49.5 us; the launch traced here: 49.3 us
  Pallas kernels  45.7 us (92%)
  local copies, waits for them, and re-layouts  2.93 us (6%)
  between operations  0.65 us (1%)
    pallas_call x1, Pallas kernels, per_device(): pl.pallas_call(functools.partial(kernel, counts), out_shape=(jax.ShapeDty...  45.7 us
    unnamed x7, local copies, waits for them, and re-layouts  2.93 us

profile of v2, /device:TPU:0, one launch (start us, length us, event | category | flops | bytes accessed | tf_op | source)
XLA Modules:
  0.0 49.3 jit_solution(17882230644491614337)
XLA Ops:
  0.6 45.7 %shard_map.94 = (f32[3,16,512]{2,1,0:T(8,128)}, f32[16,512]{1,0:T(8,128)}, f32[16,512]{1,0:T(8,128)}) custom-call(f32[3,16,512]{2,1,0:T(8,128)} %bitcast.5, f32[16,512]{1,0:T(8,128)} %bitcast.7, s32[16]{0:T(128)} %place_ref.1, f32[104,128]{1,0:T(8,128)} %constant.8.clone.rows_ref, bf16[384,256]{1,0:T(8,128)(2,1)} %constant.9.clone.fwd_ref, ...), custom_call_target="tpu_custom_call" | custom-call | tf_op jit(solution)/shard_map/pallas_call | solution.py:539
  46.4 0.0 copy-start.1
  46.4 1.5 %copy.13 = f32[3,512,16]{1,2,0:T(8,128)} copy(f32[3,512,16]{1,2,0:T(8,128)} %bitcast.6) | data formatting | bytes 196608
  47.9 0.0 copy-done.1
  47.9 0.0 copy-start
  47.9 0.6 %copy.14 = f32[512,16]{0,1:T(8,128)} copy(f32[512,16]{0,1:T(8,128)S(1)} %bitcast.9) | data formatting | bytes 65536
  48.5 0.2 copy-done
  48.7 0.6 %copy.15 = f32[512,16]{0,1:T(8,128)} copy(f32[512,16]{0,1:T(8,128)S(1)} %bitcast.8) | data formatting | bytes 65536
Async XLA Ops:
  46.4 1.6 %copy-start.1 = (f32[16,512]{1,0:T(8,128)S(1)}, f32[16,512]{1,0:T(8,128)}, u32[]{:S(2)}) copy-start(f32[16,512]{1,0:T(8,128)} %get-tuple-element.7) | copy-start | bytes 98308
  47.9 0.8 %copy-start = (f32[16,512]{1,0:T(8,128)S(1)}, f32[16,512]{1,0:T(8,128)}, u32[]{:S(2)}) copy-start(f32[16,512]{1,0:T(8,128)} %get-tuple-element.8) | copy-start | bytes 98308

commit v3 on v2

--- a/solution.py
+++ b/solution.py
@@ -108,9 +108,7 @@
     recv_xy,
     recv_z,
     sums,
-    sums_x,
-    sums_y,
-    sums_z,
+    sums_in,
     send_sem,
     recv_sem,
     sum_send,
@@ -119,9 +117,6 @@
     f32 = jnp.float32
     me = [lax.axis_index(name) for name in AXES]
     has = [(me[i] > 0, me[i] < counts[i] - 1) for i in range(3)]
-
-    def at(axis, position):
-        return tuple(position if i == axis else me[i] for i in range(3))
 
     lane = lax.broadcasted_iota(jnp.int32, (1, 16, 128), 2)
     row = lax.broadcasted_iota(jnp.int32, (1, 16, 128), 1)
@@ -194,14 +189,26 @@
 
     directions = [
         (dx, dy, dz)
-        for dx in (-1, 1, 0)
-        for dy in (0, -1, 1)
-        for dz in (0, -1, 1)
+        for dx in (-1, 0, 1)
+        for dy in (-1, 0, 1)
+        for dz in (-1, 0, 1)
         if (dx, dy, dz) != (0, 0, 0)
     ]
+    columns = [(dx, dy) for dx in (-1, 1, 0) for dy in (0, -1, 1)]
+    cases = []
+    if counts[2] > 2:
+        cases.append(((-1, 0, 1), jnp.logical_and(has[2][0], has[2][1])))
+    if counts[2] > 1:
+        cases.append(((-1, 0), jnp.logical_not(has[2][1])))
+        cases.append(((0, 1), jnp.logical_not(has[2][0])))
+    else:
+        cases.append(((0,), me[2] == 0))
 
     def code(d):
         return (d[0] + 1) * 9 + (d[1] + 1) * 3 + d[2] + 1
+
+    def group(d):
+        return (d[0] + 1) * 3 + d[1] + 1 if d[0] or d[1] else 9 + side_of(d[2])
 
     def exists(d):
         flag = None
@@ -231,48 +238,93 @@
         return pltpu.make_async_remote_copy(
             src_ref=source(r, d, c),
             dst_ref=target(r, back, c),
-            send_sem=send_sem.at[r, code(d)],
-            recv_sem=recv_sem.at[r, code(back)],
+            send_sem=send_sem.at[group(d)],
+            recv_sem=recv_sem.at[r, group(back)],
             device_id=tuple(me[i] + d[i] for i in range(3)),
             device_id_type=MESH,
         )
 
-    def start(r, c, chosen):
-        for d in chosen:
-
-            @pl.when(exists(d))
+    def each_column(act):
+        for steps, flag in cases:
+
+            @pl.when(flag)
             def _():
-                copy(r, d, c, False).start()
+                for dx, dy in columns:
+                    if dx or dy:
+
+                        @pl.when(exists((dx, dy, 0)))
+                        def _():
+                            act(dx, dy, steps)
+
+                    else:
+                        act(dx, dy, [dz for dz in steps if dz])
+
+    def start(r, c):
+        def act(dx, dy, steps):
+            for dz in steps:
+                copy(r, (dx, dy, dz), c, False).start()
+
+        each_column(act)
+
+    def whole(ref, d, rounds_sem):
+        return pltpu.make_async_remote_copy(
+            src_ref=ref,
+            dst_ref=ref,
+            send_sem=send_sem.at[group(d)],
+            recv_sem=rounds_sem.at[group(d)],
+            device_id=tuple(me[i] + d[i] for i in range(3)),
+            device_id_type=MESH,
+        )
 
     def finish(r, c):
-        for d in directions:
-
-            @pl.when(exists(d))
-            def _():
-                copy(r, d, c, True).wait_recv()
+        def act(dx, dy, steps):
+            if dx or dy:
+                d = (dx, dy, 0)
+                ref = recv_xy.at[r, pl.ds(code((dx, dy, steps[0])), len(steps))]
+                whole(ref, d, recv_sem.at[r]).wait_recv()
+            else:
+                for dz in steps:
+                    copy(r, (0, 0, dz), c, True).wait_recv()
+
+        each_column(act)
+
+    def sent():
+        def act(dx, dy, steps):
+            if dx or dy:
+                d = (dx, dy, 0)
+                ref = recv_xy.at[:, pl.ds(code((dx, dy, steps[0])), len(steps))]
+                whole(ref, d, recv_sem.at[0]).wait_send()
+            else:
+                for dz in steps:
+                    whole(recv_z.at[pl.ds(0, 2)], (0, 0, dz), recv_sem.at[0]).wait_send()
+
+        each_column(act)
+
+    def each_other(act):
+        for kx in range(counts[0]):
+            for ky in range(counts[1]):
+                base = (kx * counts[1] + ky) * counts[2]
+                first = 0 if base else 1
+
+                def one(kz, _):
+                    steps = (kx, ky, kz)
+                    device = tuple(lax.rem(me[i] + steps[i], counts[i]) for i in range(3))
+                    act(device, base + kz - 1)
+                    return 0
+
+                if counts[2] <= 8:
+                    for kz in range(first, counts[2]):
+                        one(kz, 0)
+                else:
+                    lax.fori_loop(first, counts[2], one, 0)
 
     barrier = pltpu.get_barrier_semaphore()
-    for d in directions:
-
-        @pl.when(exists(d))
-        def _():
-            pl.semaphore_signal(
-                barrier,
-                inc=1,
-                device_id=tuple(me[i] + d[i] for i in range(3)),
-                device_id_type=MESH,
-            )
-
-    for axis in range(3):
-        for k in range(1, counts[axis]):
-            pl.semaphore_signal(
-                barrier,
-                inc=1,
-                device_id=at(axis, lax.rem(me[axis] + k, counts[axis])),
-                device_id_type=MESH,
-            )
-    near = [1 + (me[i] > 0).astype(jnp.int32) + (me[i] < counts[i] - 1).astype(jnp.int32) for i in range(3)]
-    greeted = near[0] * near[1] * near[2] - 1 + sum(n - 1 for n in counts)
+
+    def greet(device, index):
+        pl.semaphore_signal(barrier, inc=1, device_id=device, device_id_type=MESH)
+
+    each_other(greet)
+    others = counts[0] * counts[1] * counts[2] - 1
     for d in directions:
 
         @pl.when(jnp.logical_not(exists(d)))
@@ -300,16 +352,13 @@
             x = turn(x, 64, 1)
         return x
 
-    def nothing():
-        return None
-
     def z_joined(r, dx, dy):
         mid = recv_xy[r, code((dx, dy, 0))]
         low = turn(recv_xy[r, code((dx, dy, -1))], -7, 1)
         high = turn(recv_xy[r, code((dx, dy, 1))], 7, 1)
         return mid + jnp.where(c8 == 0, low, jnp.where(c8 == 7, high, 0.0))
 
-    def assemble(v, r, between=nothing):
+    def assemble(v, r):
         v = list(v)
         c = v[0].shape[0]
         lower, upper = turn(v[0], 64, 2), turn(v[3], 64, 2)
@@ -337,7 +386,6 @@
                 part = requarter(v[3 * side][k, 8 * side : 8 * side + 8], k, base)
                 acc = part if acc is None else jnp.where(quarter == k, part, acc)
             send_x[r, side] = acc
-        start(r, c, [d for d in directions if d[0]])
         for side, face in ((0, lower), (1, upper)):
             acc = None
             for k in range(c):
@@ -345,7 +393,6 @@
                 part = turn(part, k + 5 * side, 0)
                 acc = part if acc is None else jnp.where(y8 == k, part, acc)
             send_y[r, side] = acc
-        start(r, c, [d for d in directions if not d[0] and d[1]])
         lower = v[0]
         upper = turn(v[0], -7, 2)
         for t in range(1, 4):
@@ -354,8 +401,7 @@
         for side, face in ((0, lower), (1, upper)):
             for k in range(c):
                 send_z[r, side, k] = jnp.where(c8 < 4, face[k, 0:8], turn(face[k, 8:16], 4, 1))
-        start(r, c, [d for d in directions if not d[0] and not d[1]])
-        between()
+        start(r, c)
         finish(r, c)
         for side in range(2):
             dx = 2 * side - 1
@@ -404,7 +450,7 @@
     square_x = along_x(64, mobile)
     square_yz = along_lanes(mobile, sqr_ref)
     diag = [mass_shift * quad[t] + square_x[t] + square_yz[t] for t in range(4)]
-    pl.semaphore_wait(barrier, greeted)
+    pl.semaphore_wait(barrier, others)
     joint = assemble([jnp.concatenate([first[t], diag[t]], axis=0) for t in range(4)], 0)
     inverse_jacobi = [1.0 / joint[t][3:4] for t in range(4)]
     k1 = [joint[t][0:3] * share[t] for t in range(4)]
@@ -456,39 +502,36 @@
     lw = local(w)
     delta_row = dot_row(s, w, share)
     eps_row = dot_row(w, lw)
-    sums[0] = jnp.concatenate(
+    partial = jnp.concatenate(
         [rho_row, gamma_row, delta_row, eps_row, jnp.zeros((4, 128), f32)], axis=0
     )
-    sum_bufs = (sums_x, sums_y, sums_z)
-
-    def sum_copy(axis, k):
-        return pltpu.make_async_remote_copy(
-            src_ref=sums.at[axis],
-            dst_ref=sum_bufs[axis].at[k - 1],
-            send_sem=sum_send[axis].at[k - 1],
-            recv_sem=sum_recv[axis].at[k - 1],
-            device_id=at(axis, lax.rem(me[axis] + k, counts[axis])),
+    partial = jnp.sum(partial, axis=1, keepdims=True)
+    own = jnp.sum(jnp.where(sub8 == lane8, partial, 0.0), axis=0, keepdims=True)
+    sums[...] = own
+
+    def share_sums(device, index):
+        pltpu.make_async_remote_copy(
+            src_ref=sums,
+            dst_ref=sums_in.at[index],
+            send_sem=sum_send,
+            recv_sem=sum_recv,
+            device_id=device,
             device_id_type=MESH,
-        )
-
-    def sum_start(axis):
-        for k in range(1, counts[axis]):
-            sum_copy(axis, k).start()
-
-    def sum_finish(axis):
-        joined = sums[axis]
-        for k in range(1, counts[axis]):
-            sum_copy(axis, k).wait_recv()
-            joined = joined + sum_bufs[axis][k - 1]
-        sums[axis + 1] = joined
-
-    def reduce_sums():
-        for axis in range(3):
-            sum_start(axis)
-            sum_finish(axis)
-
-    t_vec = assemble(lw, 6, reduce_sums)
-    four = jnp.sum(sums[3], axis=1, keepdims=True)
+        ).start()
+
+    each_other(share_sums)
+    t_vec = assemble(lw, 6)
+    arrived = pltpu.make_async_remote_copy(
+        src_ref=sums_in,
+        dst_ref=sums_in,
+        send_sem=sum_send,
+        recv_sem=sum_recv,
+        device_id=tuple(lax.rem(me[i] + 1, counts[i]) for i in range(3)),
+        device_id_type=MESH,
+    )
+    arrived.wait_recv()
+    joined = own + jnp.sum(sums_in[...], axis=0)
+    four = jnp.sum(jnp.where(sub8 == lane8, joined, 0.0), axis=1, keepdims=True)
     rho, gamma, delta, eps = (four[i : i + 1].reshape(1, 1, 1) for i in range(4))
     alpha0 = rho / gamma
     rho1 = rho - 2.0 * alpha0 * gamma + alpha0 * alpha0 * delta
@@ -513,17 +556,8 @@
             [(r0[t] - along * s[t] + side_step * t_vec[t])[0] for t in range(4)], axis=1
         )
     )
-    for r in range(ROUNDS):
-        c = 4 if r == 0 else 3 if r < 4 else 1
-        for d in directions:
-
-            @pl.when(exists(d))
-            def _():
-                copy(r, d, c, False).wait_send()
-
-    for axis in range(3):
-        for k in range(1, counts[axis]):
-            sum_copy(axis, k).wait_send()
+    sent()
+    arrived.wait_send()
 
 
 def per_device(counts, velocity, inv_density, element_place):
@@ -535,7 +569,7 @@
     faces = pltpu.VMEM((ROUNDS, 2, 8, 128), f32)
     faces_z = pltpu.VMEM((ROUNDS, 2, 4, 8, 128), f32)
     dma = pltpu.SemaphoreType.DMA
-    peers = [n - 1 for n in counts]
+    others = counts[0] * counts[1] * counts[2] - 1
     advected, pressure, residual = pl.pallas_call(
         functools.partial(kernel, counts),
         out_shape=(
@@ -551,14 +585,12 @@
             faces_z,
             pltpu.VMEM((ROUNDS, 27, 8, 128), f32),
             faces_z,
-            pltpu.VMEM((4, 8, 128), f32),
-            pltpu.VMEM((peers[0], 8, 128), f32),
-            pltpu.VMEM((peers[1], 8, 128), f32),
-            pltpu.VMEM((peers[2], 8, 128), f32),
-            dma((ROUNDS, 27)),
-            dma((ROUNDS, 27)),
-            [dma((n,)) for n in peers],
-            [dma((n,)) for n in peers],
+            pltpu.VMEM((1, 128), f32),
+            pltpu.VMEM((others, 1, 128), f32),
+            dma((11,)),
+            dma((ROUNDS, 11)),
+            dma,
+            dma,
         ],
         compiler_params=pltpu.CompilerParams(collective_id=0, has_side_effects=True),
     )(

time: 49.5 us -> 43.1 us (0.87)
  Pallas kernels: 45.7 us -> 39.2 us
    pallas_call x1, Pallas kernels: 45.7 us -> 39.2 us  [per_device(): pl.pallas_call(functools.partial(kernel, counts), out_shape=(jax.ShapeDty...]
where the time goes in v3:
time: 43.1 us; the launch traced here: 42.8 us
  Pallas kernels  39.2 us (91%)
  local copies, waits for them, and re-layouts  2.93 us (7%)
  between operations  0.65 us (2%)
    pallas_call x1, Pallas kernels, per_device(): pl.pallas_call(functools.partial(kernel, counts), out_shape=(jax.ShapeDty...  39.2 us
    unnamed x7, local copies, waits for them, and re-layouts  2.93 us

profile of v3, /device:TPU:0, one launch (start us, length us, event | category | flops | bytes accessed | tf_op | source)
XLA Modules:
  0.0 42.8 jit_solution(9041704786937828965)
XLA Ops:
  0.6 39.2 %shard_map.94 = (f32[3,16,512]{2,1,0:T(8,128)}, f32[16,512]{1,0:T(8,128)}, f32[16,512]{1,0:T(8,128)}) custom-call(f32[3,16,512]{2,1,0:T(8,128)} %bitcast.5, f32[16,512]{1,0:T(8,128)} %bitcast.7, s32[16]{0:T(128)} %place_ref.1, f32[104,128]{1,0:T(8,128)} %constant.8.clone.rows_ref, bf16[384,256]{1,0:T(8,128)(2,1)} %constant.9.clone.fwd_ref, ...), custom_call_target="tpu_custom_call" | custom-call | tf_op jit(solution)/shard_map/pallas_call | solution.py:573
  39.9 0.0 copy-start.1
  39.9 1.5 %copy.13 = f32[3,512,16]{1,2,0:T(8,128)} copy(f32[3,512,16]{1,2,0:T(8,128)} %bitcast.6) | data formatting | bytes 196608
  41.4 0.0 copy-done.1
  41.4 0.0 copy-start
  41.4 0.6 %copy.14 = f32[512,16]{0,1:T(8,128)} copy(f32[512,16]{0,1:T(8,128)S(1)} %bitcast.9) | data formatting | bytes 65536
  42.1 0.2 copy-done
  42.2 0.6 %copy.15 = f32[512,16]{0,1:T(8,128)} copy(f32[512,16]{0,1:T(8,128)S(1)} %bitcast.8) | data formatting | bytes 65536
Async XLA Ops:
  39.9 1.6 %copy-start.1 = (f32[16,512]{1,0:T(8,128)S(1)}, f32[16,512]{1,0:T(8,128)}, u32[]{:S(2)}) copy-start(f32[16,512]{1,0:T(8,128)} %get-tuple-element.7) | copy-start | bytes 98308
  41.4 0.8 %copy-start = (f32[16,512]{1,0:T(8,128)S(1)}, f32[16,512]{1,0:T(8,128)}, u32[]{:S(2)}) copy-start(f32[16,512]{1,0:T(8,128)} %get-tuple-element.8) | copy-start | bytes 98308

commit v4 on v3

--- a/solution.py
+++ b/solution.py
@@ -118,6 +118,32 @@
     me = [lax.axis_index(name) for name in AXES]
     has = [(me[i] > 0, me[i] < counts[i] - 1) for i in range(3)]
 
+    def each_other(act):
+        for kx in range(counts[0]):
+            for ky in range(counts[1]):
+                base = (kx * counts[1] + ky) * counts[2]
+                first = 0 if base else 1
+
+                def one(kz, _):
+                    steps = (kx, ky, kz)
+                    device = tuple(lax.rem(me[i] + steps[i], counts[i]) for i in range(3))
+                    act(device, base + kz - 1)
+                    return 0
+
+                if counts[2] <= 8:
+                    for kz in range(first, counts[2]):
+                        one(kz, 0)
+                else:
+                    lax.fori_loop(first, counts[2], one, 0)
+
+    barrier = pltpu.get_barrier_semaphore()
+
+    def greet(device, index):
+        pl.semaphore_signal(barrier, inc=1, device_id=device, device_id_type=MESH)
+
+    each_other(greet)
+    others = counts[0] * counts[1] * counts[2] - 1
+
     lane = lax.broadcasted_iota(jnp.int32, (1, 16, 128), 2)
     row = lax.broadcasted_iota(jnp.int32, (1, 16, 128), 1)
     ex, ey = row // BY, row % BY
@@ -300,31 +326,6 @@
 
         each_column(act)
 
-    def each_other(act):
-        for kx in range(counts[0]):
-            for ky in range(counts[1]):
-                base = (kx * counts[1] + ky) * counts[2]
-                first = 0 if base else 1
-
-                def one(kz, _):
-                    steps = (kx, ky, kz)
-                    device = tuple(lax.rem(me[i] + steps[i], counts[i]) for i in range(3))
-                    act(device, base + kz - 1)
-                    return 0
-
-                if counts[2] <= 8:
-                    for kz in range(first, counts[2]):
-                        one(kz, 0)
-                else:
-                    lax.fori_loop(first, counts[2], one, 0)
-
-    barrier = pltpu.get_barrier_semaphore()
-
-    def greet(device, index):
-        pl.semaphore_signal(barrier, inc=1, device_id=device, device_id_type=MESH)
-
-    each_other(greet)
-    others = counts[0] * counts[1] * counts[2] - 1
     for d in directions:
 
         @pl.when(jnp.logical_not(exists(d)))
@@ -358,7 +359,7 @@
         high = turn(recv_xy[r, code((dx, dy, 1))], 7, 1)
         return mid + jnp.where(c8 == 0, low, jnp.where(c8 == 7, high, 0.0))
 
-    def assemble(v, r):
+    def assemble(v, r, hook=None):
         v = list(v)
         c = v[0].shape[0]
         lower, upper = turn(v[0], 64, 2), turn(v[3], 64, 2)
@@ -402,6 +403,8 @@
             for k in range(c):
                 send_z[r, side, k] = jnp.where(c8 < 4, face[k, 0:8], turn(face[k, 8:16], 4, 1))
         start(r, c)
+        if hook is not None:
+            hook()
         finish(r, c)
         for side in range(2):
             dx = 2 * side - 1
@@ -447,17 +450,26 @@
         ]
 
     first = advect(velocity)
-    square_x = along_x(64, mobile)
-    square_yz = along_lanes(mobile, sqr_ref)
-    diag = [mass_shift * quad[t] + square_x[t] + square_yz[t] for t in range(4)]
+    diag = []
+
+    def diagonal():
+        square_x = along_x(64, mobile)
+        square_yz = along_lanes(mobile, sqr_ref)
+        diag.extend(mass_shift * quad[t] + square_x[t] + square_yz[t] for t in range(4))
+
     pl.semaphore_wait(barrier, others)
-    joint = assemble([jnp.concatenate([first[t], diag[t]], axis=0) for t in range(4)], 0)
-    inverse_jacobi = [1.0 / joint[t][3:4] for t in range(4)]
-    k1 = [joint[t][0:3] * share[t] for t in range(4)]
+    first = assemble(first, 0, diagonal)
+    k1 = [first[t] * share[t] for t in range(4)]
     total_rate = k1
     v = [velocity[t] - (0.5 * time_step) * k1[t] for t in range(4)]
     for r, step, weight in ((1, 0.5, 2.0), (2, 1.0, 2.0), (3, 0.0, 1.0)):
-        g = assemble(advect(v), r)
+        g = advect(v)
+        if r == 1:
+            g = assemble([jnp.concatenate([g[t], diag[t]], axis=0) for t in range(4)], r)
+            inverse_jacobi = [1.0 / g[t][3:4] for t in range(4)]
+            g = [g[t][0:3] for t in range(4)]
+        else:
+            g = assemble(g, r)
         g = [g[t] * share[t] for t in range(4)]
         total_rate = [total_rate[t] + weight * g[t] for t in range(4)]
         if step:
@@ -467,7 +479,14 @@
     dx = along_x(0, [advected[t][0:1] for t in range(4)])
     dyz = along_lanes([advected[t][1:3] for t in range(4)], fwd_ref)
     div = [dx[t] + dyz[t][0:1, :, :128] + dyz[t][1:2, :, 128:] for t in range(4)]
-    total_div = assemble(div, 4)
+    def put(field):
+        return order(to_slot, field)
+
+    def put_advected():
+        for i in range(3):
+            adv_ref[i] = put(jnp.concatenate([advected[t][i] for t in range(4)], axis=1))
+
+    total_div = assemble(div, 4, put_advected)
     r0 = [total_div[t] * (quad[t] * (-1.0 / time_step)) for t in range(4)]
 
     def local(v):
@@ -543,11 +562,6 @@
     along = alpha0 + alpha1 * (1.0 + beta)
     side_step = alpha0 * alpha1
 
-    def put(field):
-        return order(to_slot, field)
-
-    for i in range(3):
-        adv_ref[i] = put(jnp.concatenate([advected[t][i] for t in range(4)], axis=1))
     pre_ref[...] = put(
         jnp.concatenate([(along * z0[t] - side_step * w[t])[0] for t in range(4)], axis=1)
     )
@@ -558,6 +572,12 @@
     )
     sent()
     arrived.wait_send()
+
+
+def finish_kernel(adv_ref, pre_ref, res_ref, adv_out, pre_out, res_out):
+    adv_out[...] = adv_ref[...]
+    pre_out[...] = pre_ref[...]
+    res_out[...] = res_ref[...]
 
 
 def per_device(counts, velocity, inv_density, element_place):
@@ -570,13 +590,14 @@
     faces_z = pltpu.VMEM((ROUNDS, 2, 4, 8, 128), f32)
     dma = pltpu.SemaphoreType.DMA
     others = counts[0] * counts[1] * counts[2] - 1
-    advected, pressure, residual = pl.pallas_call(
+    shapes = (
+        jax.ShapeDtypeStruct((3, elements, points), f32),
+        jax.ShapeDtypeStruct((elements, points), f32),
+        jax.ShapeDtypeStruct((elements, points), f32),
+    )
+    computed = pl.pallas_call(
         functools.partial(kernel, counts),
-        out_shape=(
-            jax.ShapeDtypeStruct((3, elements, points), f32),
-            jax.ShapeDtypeStruct((elements, points), f32),
-            jax.ShapeDtypeStruct((elements, points), f32),
-        ),
+        out_shape=shapes,
         in_specs=[vmem, vmem, pl.BlockSpec(memory_space=pltpu.SMEM), vmem, vmem, vmem, vmem],
         out_specs=(vmem, vmem, vmem),
         scratch_shapes=[
@@ -602,6 +623,12 @@
         jnp.asarray(backward),
         jnp.asarray(square),
     )
+    advected, pressure, residual = pl.pallas_call(
+        finish_kernel,
+        out_shape=shapes,
+        in_specs=[vmem, vmem, vmem],
+        out_specs=(vmem, vmem, vmem),
+    )(*computed)
     return advected.transpose(0, 2, 1), pressure.T, residual.T
 
 

time: 43.1 us -> 41.5 us (0.963)
  local copies, waits for them, and re-layouts: 2.93 us -> 0 us
  Pallas kernels: 39.2 us -> 40.7 us
    unnamed x7 -> x0, local copies, waits for them, and re-layouts: 2.93 us -> none
    pallas_call x1 -> x2, Pallas kernels: 39.2 us -> 40.7 us  [the longest x1 39.1 us: per_device(): pl.pallas_call(functools.partial(kernel, counts), out_shape=shapes, in_sp...]
where the time goes in v4:
time: 41.5 us; the launch traced here: 41.3 us
  Pallas kernels  40.7 us (98%)
  between operations  0.64 us (2%)
    pallas_call x1, Pallas kernels, per_device(): pl.pallas_call(functools.partial(kernel, counts), out_shape=shapes, in_sp...  39.1 us
    pallas_call x1, Pallas kernels, per_device(): pl.pallas_call(finish_kernel, out_shape=shapes, in_specs=[vmem, vmem, vme...  1.58 us

profile of v4, /device:TPU:0, one launch (start us, length us, event | category | flops | bytes accessed | tf_op | source)
XLA Modules:
  0.0 41.3 jit_solution(13617429323750535658)
XLA Ops:
  0.6 39.1 %shard_map.94 = (f32[3,16,512]{2,1,0:T(8,128)}, f32[16,512]{1,0:T(8,128)}, f32[16,512]{1,0:T(8,128)}) custom-call(f32[3,16,512]{2,1,0:T(8,128)} %bitcast.5, f32[16,512]{1,0:T(8,128)} %bitcast.6, s32[16]{0:T(128)} %place_ref.1, f32[104,128]{1,0:T(8,128)} %constant.8.clone.rows_ref, bf16[384,256]{1,0:T(8,128)(2,1)} %constant.9.clone.fwd_ref, ...), custom_call_target="tpu_custom_call" | custom-call | tf_op jit(solution)/shard_map/pallas_call | solution.py:598
  39.8 1.6 %shard_map.95 = (f32[3,16,512]{2,1,0:T(8,128)}, f32[16,512]{1,0:T(8,128)}, f32[16,512]{1,0:T(8,128)}) custom-call(f32[3,16,512]{2,1,0:T(8,128)} %get-tuple-element.9.adv_ref, f32[16,512]{1,0:T(8,128)} %get-tuple-element.10.pre_ref, f32[16,512]{1,0:T(8,128)} %get-tuple-element.11.res_ref), custom_call_target="tpu_custom_call" | custom-call | tf_op jit(solution)/shard_map/pallas_call | solution.py:626
